TPU v7x, 32 devices: a whole 2x2x4 slice. The times are simulated.
32 devices in a mesh: gx: 4 (over y, x), gy: 2 (over core), gz: 4 (over z).
Axes of the slice: x: 2, y: 2, z: 4, core: 2. Of those that a mesh axis runs over, the one named last changes fastest.
Arguments:
- old_pos: float32 [3, 4, 2, 4, 1536], P(None, 'gx', 'gy', 'gz'), may hold values from -6 to 6
- displacement: float32 [3, 4, 2, 4, 1536], P(None, 'gx', 'gy', 'gz'), may hold values from -0.3 to 0.3
- inv_mass: float32 [4, 2, 4, 1536], P('gx', 'gy', 'gz'), may hold values from 0.0625 to 1
- bond_head: int32 [4, 2, 4, 1024], P('gx', 'gy', 'gz'), may hold values from 0 to 1535, as said below
- bond_tail: int32 [4, 2, 4, 1024], P('gx', 'gy', 'gz'), may hold values from 0 to 1967, as said below
- send_list: int32 [4, 2, 4, 16], P('gx', 'gy', 'gz'), may hold values from 0 to 1535, as said below
Outputs:
- new_pos: float32 [3, 4, 2, 4, 1536], P(None, 'gx', 'gy', 'gz')
- multipliers: float32 [4, 2, 4, 1024], P('gx', 'gy', 'gz')
Inputs may be any that keep to these rules, and one draw needn't show every extreme that they name: `bond_head`: distinct atoms of the owning domain; no atom is the first atom of two constraints. `bond_tail`: below 1536: an atom of the owning domain other than the constraint's first atom, never in send_list; otherwise a slot 1536 + block * 16 + entry with block in 0..26 other than 13, distinct within a domain; 192 constraints of each domain use such slots. `send_list`: distinct atoms of the domain; a send atom is never a constraint's first atom and never a local second atom.
All inputs are finite; a program needn't handle non-finite values.
Results may differ from a plain program's by a relative error of at most 0.0011.
Values sent between devices are 32-bit elements; how exact they have to be, the bound alone decides.
No kernel may reach another device: no remote copies, remote signals or barrier semaphores. Data moves between devices by JAX's collectives and lax.ppermute only.
A program may use at most 64 MiB of HBM per device.

v0:
```python
import jax
import jax.numpy as jnp
from jax import lax
from jax.sharding import PartitionSpec as P

ORDER = 4


def with_halo(value, sides, width):
    for axis, dim in sides:
        devices, length = (lax.axis_size(axis), value.shape[dim])
        up = [(i, (i + 1) % devices) for i in range(devices)]
        down = [(j, i) for i, j in up]
        last = lax.slice_in_dim(value, length - width, length, axis=dim)
        leading = lax.slice_in_dim(value, 0, width, axis=dim)
        before = lax.ppermute(last, axis, up)
        after = lax.ppermute(leading, axis, down)
        value = jnp.concatenate([before, value, after], axis=dim)
    return value


def gather_back(returned):
    widened = with_halo(returned, (("gx", 1), ("gy", 2), ("gz", 3)), 1)
    return jnp.sum(widened[:, ::2, ::2, ::2, :], axis=(1, 2, 3))


def per_device(old_pos, displacement, inv_mass, bond_head, bond_tail, send_list):
    atom_count = old_pos.shape[-1]
    bond_count = bond_head.shape[-1]
    send_count = send_list.shape[-1]
    old_local = old_pos.reshape(3, atom_count)
    move_local = displacement.reshape(3, atom_count)
    mass_local = inv_mass.reshape(1, atom_count)
    head_atom = bond_head.reshape(bond_count)
    tail_atom = bond_tail.reshape(bond_count)
    outbound = send_list.reshape(send_count)
    wide_count = 27 * send_count
    packed = jnp.concatenate(
        [old_local[:, outbound], move_local[:, outbound], mass_local[:, outbound]], axis=0
    )
    arrived = with_halo(
        packed.reshape(7, 1, 1, 1, send_count), (("gx", 1), ("gy", 2), ("gz", 3)), 1
    )
    arrived = arrived.reshape(7, wide_count)
    pos_local = old_local + move_local
    ext_old = jnp.concatenate([old_local, arrived[0:3]], axis=1)
    ext_new = jnp.concatenate([pos_local, arrived[0:3] + arrived[3:6]], axis=1)
    ext_mass = jnp.concatenate([mass_local, arrived[6:7]], axis=1)
    bond_old = ext_old[:, head_atom] - ext_old[:, tail_atom]
    length = jnp.maximum(jnp.sqrt(jnp.sum(bond_old * bond_old, axis=0)), 0.5)
    direction = bond_old / length
    bond_scale = 1.0 / jnp.sqrt(ext_mass[0, head_atom] + ext_mass[0, tail_atom])

    def spread(values):
        weighted = bond_scale * values * direction
        buffer = jnp.zeros((3, atom_count + wide_count), jnp.float32)
        buffer = buffer.at[:, head_atom].add(weighted).at[:, tail_atom].add(-weighted)
        incoming = gather_back(buffer[:, atom_count:].reshape(3, 3, 3, 3, send_count))
        local_sum = buffer[:, :atom_count].at[:, outbound].add(incoming)
        return mass_local * local_sum

    def couple(values):
        shift_vec = spread(values)
        remote = with_halo(
            shift_vec[:, outbound].reshape(3, 1, 1, 1, send_count),
            (("gx", 1), ("gy", 2), ("gz", 3)),
            1,
        )
        extended = jnp.concatenate([shift_vec, remote.reshape(3, wide_count)], axis=1)
        return values - bond_scale * jnp.sum(
            direction * (extended[:, head_atom] - extended[:, tail_atom]), axis=0
        )

    def expand(right_side):
        solution = right_side
        series = right_side
        for sweep in range(ORDER):
            series = couple(series)
            solution = solution + series
        return solution

    right_one = bond_scale * (
        jnp.sum(direction * (ext_new[:, head_atom] - ext_new[:, tail_atom]), axis=0) - length
    )
    sol_one = expand(right_one)
    pos_local = pos_local - spread(sol_one)
    moved = with_halo(
        pos_local[:, outbound].reshape(3, 1, 1, 1, send_count), (("gx", 1), ("gy", 2), ("gz", 3)), 1
    )
    ext_moved = jnp.concatenate([pos_local, moved.reshape(3, wide_count)], axis=1)
    stretch = ext_moved[:, head_atom] - ext_moved[:, tail_atom]
    current = jnp.sum(stretch * stretch, axis=0)
    target = jnp.sqrt(jnp.maximum(2.0 * length * length - current, 0.5 * length * length))
    sol_two = expand(bond_scale * (length - target))
    pos_local = pos_local - spread(sol_two)
    return (pos_local.reshape(old_pos.shape), (sol_one + sol_two).reshape(bond_head.shape))


def solution(mesh):
    return jax.shard_map(
        per_device,
        mesh=mesh,
        in_specs=(
            P(None, "gx", "gy", "gz", None),
            P(None, "gx", "gy", "gz", None),
            P("gx", "gy", "gz", None),
            P("gx", "gy", "gz", None),
            P("gx", "gy", "gz", None),
            P("gx", "gy", "gz", None),
        ),
        out_specs=(P(None, "gx", "gy", "gz", None), P("gx", "gy", "gz", None)),
        check_vma=False,
    )
```

profile of v0, /device:TPU:0, one launch (start us, length us, event | category | flops | bytes accessed | tf_op | source)
XLA Modules:
  0.0 540.6 jit_solution(5825422829706087112)
XLA Ops:
  4.2 3.0 collective-permute-start
  18.5 2.8 gather_fusion.5
  21.4 4.0 gather_fusion.6
  25.7 4.0 gather_fusion.8
  29.7 4.0 gather_fusion.7
  33.9 6.5 %gather_fusion.4 = f32[1024]{0:T(1024)S(1)} fusion(f32[1,1968]{1,0:T(1,128)S(1)} %pad_maximum_fusion.83, s32[1024]{0:T(1024)S(1)} %bitcast.84), kind=kCustom, calls=%fused_computation.4 | custom fusion | bytes 16384 | tf_op jit(solution)/shard_map/gather | solution.py:52
  40.4 6.5 %gather_fusion.3 = f32[1024]{0:T(1024)S(1)} fusion(f32[1,1968]{1,0:T(1,128)S(1)} %pad_maximum_fusion.83, s32[1024]{0:T(1024)S(1)} %bitcast.85), kind=kCustom, calls=%fused_computation.3 | custom fusion | bytes 16384 | tf_op jit(solution)/shard_map/gather | solution.py:52
  48.5 6.9 %scatter_custom_fusion = f32[3,1968]{0,1:T(8,128)S(1)} fusion(s32[1024]{0:T(1024)S(1)} %bitcast.184, f32[]{:T(128)} %constant.6.clone.1, f32[1024]{0:T(1024)S(1)} %get-tuple-element.18, f32[1024,3]{1,0:T(8,128)S(1)} %get-tuple-element.22, f32[1024]{0:T(1024)S(1)} %sqrt_maximum_fusion), kind=kCustom, calls=%fused_computation.128 | custom fusion | flops 9216 | bytes 556100 | tf_op jit(solution)/shard_map/scatter-add | solution.py:57
  55.4 7.1 %scatter_custom_fusion.1 = f32[3,1968]{0,1:T(8,128)S(1)} fusion(f32[3,1968]{0,1:T(8,128)S(1)} %scatter_custom_fusion, s32[1024]{0:T(1024)S(1)} %bitcast.173, f32[1024]{0:T(1024)S(1)} %get-tuple-element.18, f32[1024,3]{1,0:T(8,128)S(1)} %get-tuple-element.22, f32[1024]{0:T(1024)S(1)} %sqrt_maximum_fusion), kind=kCustom, calls=%fused_computation.97 | custom fusion | flops 12288 | bytes 556096 | tf_op jit(solution)/shard_map/scatter-add | solution.py:57
  71.8 2.7 collective-permute-start.11
  86.2 2.9 collective-permute-start.17
  91.9 4.0 gather_fusion.11
  96.0 4.0 gather_fusion.10
  100.4 6.9 %scatter_custom_fusion.3 = f32[3,1968]{0,1:T(8,128)S(1)} fusion(s32[1024]{0:T(1024)S(1)} %bitcast.185, f32[]{:T(128)} %constant.6.clone.1, f32[1024]{0:T(1024)S(1)} %fusion.89, f32[1024,3]{1,0:T(8,128)S(1)} %get-tuple-element.22, f32[1024]{0:T(1024)S(1)} %sqrt_maximum_fusion), kind=kCustom, calls=%fused_computation.126 | custom fusion | flops 9216 | bytes 556100 | tf_op jit(solution)/shard_map/scatter-add | solution.py:57
  107.4 7.1 %scatter_custom_fusion.4 = f32[3,1968]{0,1:T(8,128)S(1)} fusion(f32[3,1968]{0,1:T(8,128)S(1)} %scatter_custom_fusion.3, s32[1024]{0:T(1024)S(1)} %bitcast.174, f32[1024]{0:T(1024)S(1)} %fusion.89, f32[1024,3]{1,0:T(8,128)S(1)} %get-tuple-element.22, f32[1024]{0:T(1024)S(1)} %sqrt_maximum_fusion), kind=kCustom, calls=%fused_computation.95 | custom fusion | flops 12288 | bytes 556096 | tf_op jit(solution)/shard_map/scatter-add | solution.py:57
  122.8 2.9 collective-permute-start.23
  143.1 4.0 gather_fusion.14
  147.2 4.0 gather_fusion.13
  151.6 6.9 %scatter_custom_fusion.6 = f32[3,1968]{0,1:T(8,128)S(1)} fusion(s32[1024]{0:T(1024)S(1)} %bitcast.186, f32[]{:T(128)} %constant.6.clone.1, f32[1024]{0:T(1024)S(1)} %fusion.92, f32[1024,3]{1,0:T(8,128)S(1)} %get-tuple-element.22, f32[1024]{0:T(1024)S(1)} %sqrt_maximum_fusion), kind=kCustom, calls=%fused_computation.124 | custom fusion | flops 9216 | bytes 556100 | tf_op jit(solution)/shard_map/scatter-add | solution.py:57
  158.6 7.3 %scatter_custom_fusion.7 = f32[3,1968]{0,1:T(8,128)S(1)} fusion(f32[3,1968]{0,1:T(8,128)S(1)} %scatter_custom_fusion.6, s32[1024]{0:T(1024)S(1)} %bitcast.175, f32[1024]{0:T(1024)S(1)} %fusion.92, f32[1024,3]{1,0:T(8,128)S(1)} %get-tuple-element.22, f32[1024]{0:T(1024)S(1)} %sqrt_maximum_fusion), kind=kCustom, calls=%fused_computation.93 | custom fusion | flops 12288 | bytes 556096 | tf_op jit(solution)/shard_map/scatter-add | solution.py:57
  175.2 2.7 collective-permute-start.35
  189.7 2.6 collective-permute-start.41
  195.4 4.0 gather_fusion.17
  199.4 4.0 gather_fusion.16
  203.9 6.9 %scatter_custom_fusion.9 = f32[3,1968]{0,1:T(8,128)S(1)} fusion(s32[1024]{0:T(1024)S(1)} %bitcast.187, f32[]{:T(128)} %constant.6.clone.1, f32[1024]{0:T(1024)S(1)} %fusion.87, f32[1024,3]{1,0:T(8,128)S(1)} %get-tuple-element.22, f32[1024]{0:T(1024)S(1)} %sqrt_maximum_fusion), kind=kCustom, calls=%fused_computation.122 | custom fusion | flops 9216 | bytes 556100 | tf_op jit(solution)/shard_map/scatter-add | solution.py:57
  210.8 7.1 %scatter_custom_fusion.10 = f32[3,1968]{0,1:T(8,128)S(1)} fusion(f32[3,1968]{0,1:T(8,128)S(1)} %scatter_custom_fusion.9, s32[1024]{0:T(1024)S(1)} %bitcast.176, f32[1024]{0:T(1024)S(1)} %fusion.87, f32[1024,3]{1,0:T(8,128)S(1)} %get-tuple-element.22, f32[1024]{0:T(1024)S(1)} %sqrt_maximum_fusion), kind=kCustom, calls=%fused_computation.91 | custom fusion | flops 12288 | bytes 556096 | tf_op jit(solution)/shard_map/scatter-add | solution.py:57
  226.2 2.8 collective-permute-start.47
  240.8 2.9 collective-permute-start.53
  246.5 4.0 gather_fusion.20
  250.5 4.0 gather_fusion.19
  255.0 6.9 %scatter_custom_fusion.12 = f32[3,1968]{0,1:T(8,128)S(1)} fusion(s32[1024]{0:T(1024)S(1)} %bitcast.188, f32[]{:T(128)} %constant.6.clone.1, f32[1024]{0:T(1024)S(1)} %add_multiply_fusion.1, f32[1024,3]{1,0:T(8,128)S(1)} %get-tuple-element.22, f32[1024]{0:T(1024)S(1)} %sqrt_maximum_fusion), kind=kCustom, calls=%fused_computation.120 | custom fusion | flops 9216 | bytes 556100 | tf_op jit(solution)/shard_map/scatter-add | solution.py:57
  261.9 7.1 %scatter_custom_fusion.13 = f32[3,1968]{0,1:T(8,128)S(1)} fusion(f32[3,1968]{0,1:T(8,128)S(1)} %scatter_custom_fusion.12, s32[1024]{0:T(1024)S(1)} %bitcast.177, f32[1024]{0:T(1024)S(1)} %add_multiply_fusion.1, f32[1024,3]{1,0:T(8,128)S(1)} %get-tuple-element.22, f32[1024]{0:T(1024)S(1)} %sqrt_maximum_fusion), kind=kCustom, calls=%fused_computation.89 | custom fusion | flops 12288 | bytes 556096 | tf_op jit(solution)/shard_map/scatter-add | solution.py:57
  278.6 2.7 collective-permute-start.59
  283.6 2.6 scatter_fusion.4
  296.0 2.6 collective-permute-start.65
  300.7 2.8 gather_fusion.23
  303.5 4.0 gather_fusion.22
  308.8 6.9 %scatter_custom_fusion.15 = f32[3,1968]{0,1:T(8,128)S(1)} fusion(s32[1024]{0:T(1024)S(1)} %bitcast.189, f32[]{:T(128)} %constant.6.clone.1, f32[1024]{0:T(1024)S(1)} %get-tuple-element.16, f32[1024,3]{1,0:T(8,128)S(1)} %get-tuple-element.22, f32[1024]{0:T(1024)S(1)} %sqrt_maximum_fusion), kind=kCustom, calls=%fused_computation.118 | custom fusion | flops 9216 | bytes 556100 | tf_op jit(solution)/shard_map/scatter-add | solution.py:57
  315.7 7.3 %scatter_custom_fusion.16 = f32[3,1968]{0,1:T(8,128)S(1)} fusion(f32[3,1968]{0,1:T(8,128)S(1)} %scatter_custom_fusion.15, s32[1024]{0:T(1024)S(1)} %bitcast.178, f32[1024]{0:T(1024)S(1)} %get-tuple-element.16, f32[1024,3]{1,0:T(8,128)S(1)} %get-tuple-element.22, f32[1024]{0:T(1024)S(1)} %sqrt_maximum_fusion), kind=kCustom, calls=%fused_computation.87 | custom fusion | flops 12288 | bytes 556096 | tf_op jit(solution)/shard_map/scatter-add | solution.py:57
  331.2 2.7 collective-permute-start.71
  345.9 2.6 collective-permute-start.77
  350.5 2.8 gather_fusion.26
  353.4 4.0 gather_fusion.25
  358.8 6.9 %scatter_custom_fusion.18 = f32[3,1968]{0,1:T(8,128)S(1)} fusion(s32[1024]{0:T(1024)S(1)} %bitcast.190, f32[]{:T(128)} %constant.6.clone.1, f32[1024]{0:T(1024)S(1)} %fusion.90, f32[1024,3]{1,0:T(8,128)S(1)} %get-tuple-element.22, f32[1024]{0:T(1024)S(1)} %sqrt_maximum_fusion), kind=kCustom, calls=%fused_computation.116 | custom fusion | flops 9216 | bytes 556100 | tf_op jit(solution)/shard_map/scatter-add | solution.py:57
  365.7 7.1 %scatter_custom_fusion.19 = f32[3,1968]{0,1:T(8,128)S(1)} fusion(f32[3,1968]{0,1:T(8,128)S(1)} %scatter_custom_fusion.18, s32[1024]{0:T(1024)S(1)} %bitcast.179, f32[1024]{0:T(1024)S(1)} %fusion.90, f32[1024,3]{1,0:T(8,128)S(1)} %get-tuple-element.22, f32[1024]{0:T(1024)S(1)} %sqrt_maximum_fusion), kind=kCustom, calls=%fused_computation.85 | custom fusion | flops 12288 | bytes 556096 | tf_op jit(solution)/shard_map/scatter-add | solution.py:57
  382.1 2.7 collective-permute-start.83
  396.7 2.8 collective-permute-start.89
  401.3 2.8 gather_fusion.29
  404.2 4.0 gather_fusion.28
  409.6 6.9 %scatter_custom_fusion.21 = f32[3,1968]{0,1:T(8,128)S(1)} fusion(s32[1024]{0:T(1024)S(1)} %bitcast.191, f32[]{:T(128)} %constant.6.clone.1, f32[1024]{0:T(1024)S(1)} %fusion.93, f32[1024,3]{1,0:T(8,128)S(1)} %get-tuple-element.22, f32[1024]{0:T(1024)S(1)} %sqrt_maximum_fusion), kind=kCustom, calls=%fused_computation.114 | custom fusion | flops 9216 | bytes 556100 | tf_op jit(solution)/shard_map/scatter-add | solution.py:57
  416.5 7.1 %scatter_custom_fusion.22 = f32[3,1968]{0,1:T(8,128)S(1)} fusion(f32[3,1968]{0,1:T(8,128)S(1)} %scatter_custom_fusion.21, s32[1024]{0:T(1024)S(1)} %bitcast.180, f32[1024]{0:T(1024)S(1)} %fusion.93, f32[1024,3]{1,0:T(8,128)S(1)} %get-tuple-element.22, f32[1024]{0:T(1024)S(1)} %sqrt_maximum_fusion), kind=kCustom, calls=%fused_computation.83 | custom fusion | flops 12288 | bytes 556096 | tf_op jit(solution)/shard_map/scatter-add | solution.py:57
  432.1 2.7 collective-permute-start.95
  446.7 2.6 collective-permute-start.101
  451.4 2.8 gather_fusion.32
  454.2 4.0 gather_fusion.31
  459.6 6.9 %scatter_custom_fusion.24 = f32[3,1968]{0,1:T(8,128)S(1)} fusion(s32[1024]{0:T(1024)S(1)} %bitcast.192, f32[]{:T(128)} %constant.6.clone.1, f32[1024]{0:T(1024)S(1)} %fusion.88, f32[1024,3]{1,0:T(8,128)S(1)} %get-tuple-element.22, f32[1024]{0:T(1024)S(1)} %sqrt_maximum_fusion), kind=kCustom, calls=%fused_computation.112 | custom fusion | flops 9216 | bytes 556100 | tf_op jit(solution)/shard_map/scatter-add | solution.py:57
  466.6 7.3 %scatter_custom_fusion.25 = f32[3,1968]{0,1:T(8,128)S(1)} fusion(f32[3,1968]{0,1:T(8,128)S(1)} %scatter_custom_fusion.24, s32[1024]{0:T(1024)S(1)} %bitcast.181, f32[1024]{0:T(1024)S(1)} %fusion.88, f32[1024,3]{1,0:T(8,128)S(1)} %get-tuple-element.22, f32[1024]{0:T(1024)S(1)} %sqrt_maximum_fusion), kind=kCustom, calls=%fused_computation.81 | custom fusion | flops 12288 | bytes 556096 | tf_op jit(solution)/shard_map/scatter-add | solution.py:57
  483.2 2.7 collective-permute-start.107
  497.8 2.6 collective-permute-start.113
  502.5 2.8 gather_fusion.35
  505.3 4.0 gather_fusion.34
  510.7 6.9 %scatter_custom_fusion.27 = f32[3,1968]{0,1:T(8,128)S(1)} fusion(s32[1024]{0:T(1024)S(1)} %bitcast.193, f32[]{:T(128)} %constant.6.clone.1, f32[1024]{0:T(1024)S(1)} %add_multiply_fusion, f32[1024,3]{1,0:T(8,128)S(1)} %get-tuple-element.22, f32[1024]{0:T(1024)S(1)} %sqrt_maximum_fusion), kind=kCustom, calls=%fused_computation.110 | custom fusion | flops 9216 | bytes 556100 | tf_op jit(solution)/shard_map/scatter-add | solution.py:57
  517.7 7.1 %scatter_custom_fusion.28 = f32[3,1968]{0,1:T(8,128)S(1)} fusion(f32[3,1968]{0,1:T(8,128)S(1)} %scatter_custom_fusion.27, s32[1024]{0:T(1024)S(1)} %bitcast.182, f32[1024]{0:T(1024)S(1)} %add_multiply_fusion, f32[1024,3]{1,0:T(8,128)S(1)} %get-tuple-element.22, f32[1024]{0:T(1024)S(1)} %sqrt_maximum_fusion), kind=kCustom, calls=%fused_computation.79 | custom fusion | flops 12288 | bytes 556096 | tf_op jit(solution)/shard_map/scatter-add | solution.py:57
  533.0 2.7 collective-permute-start.119
  (505 shorter events, 248.4 us)
Async XLA Ops:
  4.2 5.5 %collective-permute-start = (f32[7,1,1,1,16]{4,0,3,2,1:T(8,128)S(1)}, f32[7,1,1,1,16]{4,0,3,2,1:T(8,128)S(1)}, u32[]{:S(2)}, u32[]{:S(2)}) collective-permute-start(f32[7,1,1,1,16]{4,0,3,2,1:T(8,128)S(1)} %bitcast.112), channel_id=1, source_target_pairs={{0,8},{8,16},{16,24},{24,0},{1,9},{9,17},{17,25},{25,1},{2,10},{10... | collective-permute-start | bytes 1352 | tf_op jit(solution)/shard_map/ppermute | solution.py:16
  12.1 5.9 %collective-permute-start.4 = (f32[7,3,3,1,16]{4,0,3,2,1:T(8,128)S(1)}, f32[7,3,3,1,16]{4,0,3,2,1:T(8,128)S(1)}, u32[]{:S(2)}, u32[]{:S(2)}) collective-permute-start(f32[7,3,3,1,16]{4,0,3,2,1:T(8,128)S(1)} %pad_maximum_fusion.41), channel_id=1, source_target_pairs={{0,1},{1,2},{2,3},{3,0},{4,5},{5,6},{6,7},{7,4},{8,9},{9,10},{10,1... | collective-permute-start | bytes 12104 | tf_op jit(solution)/shard_map/ppermute | solution.py:16
  13.7 4.5 collective-permute-start.5
  62.8 4.7 collective-permute-start.6
  70.6 5.8 %collective-permute-start.10 = (f32[3,5,5,1,16]{4,3,2,1,0:T(1,128)S(1)}, f32[3,5,5,1,16]{4,3,2,1,0:T(1,128)S(1)}, u32[]{:S(2)}, u32[]{:S(2)}) collective-permute-start(f32[3,5,5,1,16]{4,3,2,1,0:T(1,128)S(1)} %get-tuple-element.45), channel_id=1, source_target_pairs={{0,1},{1,2},{2,3},{3,0},{4,5},{5,6},{6,7},{7,4},{8,9},{9,10},{10,1... | collective-permute-start | bytes 14408 | tf_op jit(solution)/shard_map/ppermute | solution.py:16
  71.8 4.8 collective-permute-start.11
  78.7 4.5 collective-permute-start.12
  85.1 5.6 %collective-permute-start.16 = (f32[3,3,3,1,16]{4,0,3,2,1:T(4,128)S(1)}, f32[3,3,3,1,16]{4,0,3,2,1:T(4,128)S(1)}, u32[]{:S(2)}, u32[]{:S(2)}) collective-permute-start(f32[3,3,3,1,16]{4,0,3,2,1:T(4,128)S(1)} %pad_maximum_fusion.72), channel_id=1, source_target_pairs={{0,1},{1,2},{2,3},{3,0},{4,5},{5,6},{6,7},{7,4},{8,9},{9,10},{10,1... | collective-permute-start | bytes 5192 | tf_op jit(solution)/shard_map/ppermute | solution.py:16
  86.2 4.5 collective-permute-start.17
  114.8 4.7 collective-permute-start.18
  116.2 3.8 collective-permute-start.19
  121.6 6.1 %collective-permute-start.22 = (f32[3,5,5,1,16]{4,3,2,1,0:T(1,128)S(1)}, f32[3,5,5,1,16]{4,3,2,1,0:T(1,128)S(1)}, u32[]{:S(2)}, u32[]{:S(2)}) collective-permute-start(f32[3,5,5,1,16]{4,3,2,1,0:T(1,128)S(1)} %get-tuple-element.43), channel_id=1, source_target_pairs={{0,1},{1,2},{2,3},{3,0},{4,5},{5,6},{6,7},{7,4},{8,9},{9,10},{10,1... | collective-permute-start | bytes 14408 | tf_op jit(solution)/shard_map/ppermute | solution.py:16
  122.8 4.9 collective-permute-start.23
  129.8 4.5 collective-permute-start.24
  136.2 5.6 %collective-permute-start.28 = (f32[3,3,3,1,16]{4,0,3,2,1:T(4,128)S(1)}, f32[3,3,3,1,16]{4,0,3,2,1:T(4,128)S(1)}, u32[]{:S(2)}, u32[]{:S(2)}) collective-permute-start(f32[3,3,3,1,16]{4,0,3,2,1:T(4,128)S(1)} %pad_maximum_fusion.73), channel_id=1, source_target_pairs={{0,1},{1,2},{2,3},{3,0},{4,5},{5,6},{6,7},{7,4},{8,9},{9,10},{10,1... | collective-permute-start | bytes 5192 | tf_op jit(solution)/shard_map/ppermute | solution.py:16
  137.5 4.4 collective-permute-start.29
  166.2 4.7 collective-permute-start.30
  168.7 3.8 collective-permute-start.31
  174.0 5.9 %collective-permute-start.34 = (f32[3,5,5,1,16]{4,3,2,1,0:T(1,128)S(1)}, f32[3,5,5,1,16]{4,3,2,1,0:T(1,128)S(1)}, u32[]{:S(2)}, u32[]{:S(2)}) collective-permute-start(f32[3,5,5,1,16]{4,3,2,1,0:T(1,128)S(1)} %get-tuple-element.41), channel_id=1, source_target_pairs={{0,1},{1,2},{2,3},{3,0},{4,5},{5,6},{6,7},{7,4},{8,9},{9,10},{10,1... | collective-permute-start | bytes 14408 | tf_op jit(solution)/shard_map/ppermute | solution.py:16
  175.2 4.8 collective-permute-start.35
  182.1 4.5 collective-permute-start.36
  188.5 5.6 %collective-permute-start.40 = (f32[3,3,3,1,16]{4,0,3,2,1:T(4,128)S(1)}, f32[3,3,3,1,16]{4,0,3,2,1:T(4,128)S(1)}, u32[]{:S(2)}, u32[]{:S(2)}) collective-permute-start(f32[3,3,3,1,16]{4,0,3,2,1:T(4,128)S(1)} %pad_maximum_fusion.74), channel_id=1, source_target_pairs={{0,1},{1,2},{2,3},{3,0},{4,5},{5,6},{6,7},{7,4},{8,9},{9,10},{10,1... | collective-permute-start | bytes 5192 | tf_op jit(solution)/shard_map/ppermute | solution.py:16
  189.7 4.4 collective-permute-start.41
  218.3 4.7 collective-permute-start.42
  225.0 5.9 %collective-permute-start.46 = (f32[3,5,5,1,16]{4,3,2,1,0:T(1,128)S(1)}, f32[3,5,5,1,16]{4,3,2,1,0:T(1,128)S(1)}, u32[]{:S(2)}, u32[]{:S(2)}) collective-permute-start(f32[3,5,5,1,16]{4,3,2,1,0:T(1,128)S(1)} %get-tuple-element.39), channel_id=1, source_target_pairs={{0,1},{1,2},{2,3},{3,0},{4,5},{5,6},{6,7},{7,4},{8,9},{9,10},{10,1... | collective-permute-start | bytes 14408 | tf_op jit(solution)/shard_map/ppermute | solution.py:16
  226.2 4.8 collective-permute-start.47
  233.1 4.5 collective-permute-start.48
  239.5 5.6 %collective-permute-start.52 = (f32[3,3,3,1,16]{4,0,3,2,1:T(4,128)S(1)}, f32[3,3,3,1,16]{4,0,3,2,1:T(4,128)S(1)}, u32[]{:S(2)}, u32[]{:S(2)}) collective-permute-start(f32[3,3,3,1,16]{4,0,3,2,1:T(4,128)S(1)} %pad_maximum_fusion.75), channel_id=1, source_target_pairs={{0,1},{1,2},{2,3},{3,0},{4,5},{5,6},{6,7},{7,4},{8,9},{9,10},{10,1... | collective-permute-start | bytes 5192 | tf_op jit(solution)/shard_map/ppermute | solution.py:16
  240.8 4.4 collective-permute-start.53
  269.3 4.7 collective-permute-start.54
  271.8 3.8 collective-permute-start.55
  277.1 6.3 %collective-permute-start.58 = (f32[3,5,5,1,16]{4,3,2,1,0:T(1,128)S(1)}, f32[3,5,5,1,16]{4,3,2,1,0:T(1,128)S(1)}, u32[]{:S(2)}, u32[]{:S(2)}) collective-permute-start(f32[3,5,5,1,16]{4,3,2,1,0:T(1,128)S(1)} %get-tuple-element.37), channel_id=1, source_target_pairs={{0,1},{1,2},{2,3},{3,0},{4,5},{5,6},{6,7},{7,4},{8,9},{9,10},{10,1... | collective-permute-start | bytes 14408 | tf_op jit(solution)/shard_map/ppermute | solution.py:16
  278.6 4.8 collective-permute-start.59
  288.3 4.5 collective-permute-start.60
  294.8 5.6 %collective-permute-start.64 = (f32[3,3,3,1,16]{4,0,3,2,1:T(4,128)S(1)}, f32[3,3,3,1,16]{4,0,3,2,1:T(4,128)S(1)}, u32[]{:S(2)}, u32[]{:S(2)}) collective-permute-start(f32[3,3,3,1,16]{4,0,3,2,1:T(4,128)S(1)} %pad_maximum_fusion.76), channel_id=1, source_target_pairs={{0,1},{1,2},{2,3},{3,0},{4,5},{5,6},{6,7},{7,4},{8,9},{9,10},{10,1... | collective-permute-start | bytes 5192 | tf_op jit(solution)/shard_map/ppermute | solution.py:16
  296.0 4.4 collective-permute-start.65
  323.3 4.7 collective-permute-start.66
  324.8 3.8 collective-permute-start.67
  330.1 6.0 %collective-permute-start.70 = (f32[3,5,5,1,16]{4,3,2,1,0:T(1,128)S(1)}, f32[3,5,5,1,16]{4,3,2,1,0:T(1,128)S(1)}, u32[]{:S(2)}, u32[]{:S(2)}) collective-permute-start(f32[3,5,5,1,16]{4,3,2,1,0:T(1,128)S(1)} %get-tuple-element.35), channel_id=1, source_target_pairs={{0,1},{1,2},{2,3},{3,0},{4,5},{5,6},{6,7},{7,4},{8,9},{9,10},{10,1... | collective-permute-start | bytes 14408 | tf_op jit(solution)/shard_map/ppermute | solution.py:16
  331.2 4.8 collective-permute-start.71
  338.2 4.5 collective-permute-start.72
  344.6 5.6 %collective-permute-start.76 = (f32[3,3,3,1,16]{4,0,3,2,1:T(4,128)S(1)}, f32[3,3,3,1,16]{4,0,3,2,1:T(4,128)S(1)}, u32[]{:S(2)}, u32[]{:S(2)}) collective-permute-start(f32[3,3,3,1,16]{4,0,3,2,1:T(4,128)S(1)} %pad_maximum_fusion.77), channel_id=1, source_target_pairs={{0,1},{1,2},{2,3},{3,0},{4,5},{5,6},{6,7},{7,4},{8,9},{9,10},{10,1... | collective-permute-start | bytes 5192 | tf_op jit(solution)/shard_map/ppermute | solution.py:16
  345.9 4.4 collective-permute-start.77
  373.1 4.7 collective-permute-start.78
  380.9 6.0 %collective-permute-start.82 = (f32[3,5,5,1,16]{4,3,2,1,0:T(1,128)S(1)}, f32[3,5,5,1,16]{4,3,2,1,0:T(1,128)S(1)}, u32[]{:S(2)}, u32[]{:S(2)}) collective-permute-start(f32[3,5,5,1,16]{4,3,2,1,0:T(1,128)S(1)} %get-tuple-element.33), channel_id=1, source_target_pairs={{0,1},{1,2},{2,3},{3,0},{4,5},{5,6},{6,7},{7,4},{8,9},{9,10},{10,1... | collective-permute-start | bytes 14408 | tf_op jit(solution)/shard_map/ppermute | solution.py:16
  382.1 4.8 collective-permute-start.83
  389.0 4.5 collective-permute-start.84
  395.4 5.6 %collective-permute-start.88 = (f32[3,3,3,1,16]{4,0,3,2,1:T(4,128)S(1)}, f32[3,3,3,1,16]{4,0,3,2,1:T(4,128)S(1)}, u32[]{:S(2)}, u32[]{:S(2)}) collective-permute-start(f32[3,3,3,1,16]{4,0,3,2,1:T(4,128)S(1)} %pad_maximum_fusion.78), channel_id=1, source_target_pairs={{0,1},{1,2},{2,3},{3,0},{4,5},{5,6},{6,7},{7,4},{8,9},{9,10},{10,1... | collective-permute-start | bytes 5192 | tf_op jit(solution)/shard_map/ppermute | solution.py:16
  396.7 4.3 collective-permute-start.89
  424.0 4.7 collective-permute-start.90
  430.7 6.2 %collective-permute-start.94 = (f32[3,5,5,1,16]{4,3,2,1,0:T(1,128)S(1)}, f32[3,5,5,1,16]{4,3,2,1,0:T(1,128)S(1)}, u32[]{:S(2)}, u32[]{:S(2)}) collective-permute-start(f32[3,5,5,1,16]{4,3,2,1,0:T(1,128)S(1)} %get-tuple-element.31), channel_id=1, source_target_pairs={{0,1},{1,2},{2,3},{3,0},{4,5},{5,6},{6,7},{7,4},{8,9},{9,10},{10,1... | collective-permute-start | bytes 14408 | tf_op jit(solution)/shard_map/ppermute | solution.py:16
  432.1 4.8 collective-permute-start.95
  439.0 4.5 collective-permute-start.96
  445.5 5.6 %collective-permute-start.100 = (f32[3,3,3,1,16]{4,0,3,2,1:T(4,128)S(1)}, f32[3,3,3,1,16]{4,0,3,2,1:T(4,128)S(1)}, u32[]{:S(2)}, u32[]{:S(2)}) collective-permute-start(f32[3,3,3,1,16]{4,0,3,2,1:T(4,128)S(1)} %pad_maximum_fusion.79), channel_id=1, source_target_pairs={{0,1},{1,2},{2,3},{3,0},{4,5},{5,6},{6,7},{7,4},{8,9},{9,10},{10,1... | collective-permute-start | bytes 5192 | tf_op jit(solution)/shard_map/ppermute | solution.py:16
  446.7 4.4 collective-permute-start.101
  474.3 4.7 collective-permute-start.102
  482.0 5.9 %collective-permute-start.106 = (f32[3,5,5,1,16]{4,3,2,1,0:T(1,128)S(1)}, f32[3,5,5,1,16]{4,3,2,1,0:T(1,128)S(1)}, u32[]{:S(2)}, u32[]{:S(2)}) collective-permute-start(f32[3,5,5,1,16]{4,3,2,1,0:T(1,128)S(1)} %get-tuple-element.29), channel_id=1, source_target_pairs={{0,1},{1,2},{2,3},{3,0},{4,5},{5,6},{6,7},{7,4},{8,9},{9,10},{10,1... | collective-permute-start | bytes 14408 | tf_op jit(solution)/shard_map/ppermute | solution.py:16
  483.2 4.8 collective-permute-start.107
  490.1 4.5 collective-permute-start.108
  496.5 5.6 %collective-permute-start.112 = (f32[3,3,3,1,16]{4,0,3,2,1:T(4,128)S(1)}, f32[3,3,3,1,16]{4,0,3,2,1:T(4,128)S(1)}, u32[]{:S(2)}, u32[]{:S(2)}) collective-permute-start(f32[3,3,3,1,16]{4,0,3,2,1:T(4,128)S(1)} %pad_maximum_fusion.80), channel_id=1, source_target_pairs={{0,1},{1,2},{2,3},{3,0},{4,5},{5,6},{6,7},{7,4},{8,9},{9,10},{10,1... | collective-permute-start | bytes 5192 | tf_op jit(solution)/shard_map/ppermute | solution.py:16
  497.8 4.4 collective-permute-start.113
  525.1 4.7 collective-permute-start.114
  531.9 5.9 %collective-permute-start.118 = (f32[3,5,5,1,16]{4,3,2,1,0:T(1,128)S(1)}, f32[3,5,5,1,16]{4,3,2,1,0:T(1,128)S(1)}, u32[]{:S(2)}, u32[]{:S(2)}) collective-permute-start(f32[3,5,5,1,16]{4,3,2,1,0:T(1,128)S(1)} %get-tuple-element.27), channel_id=1, source_target_pairs={{0,1},{1,2},{2,3},{3,0},{4,5},{5,6},{6,7},{7,4},{8,9},{9,10},{10,1... | collective-permute-start | bytes 14408 | tf_op jit(solution)/shard_map/ppermute | solution.py:16
  533.0 4.8 collective-permute-start.119
  (64 other events, 125.3 us)
where the time goes:
time: 549 us; the launch traced here: 541 us
  other arithmetic  173 us (32%)
  starting transfers between devices  149 us (27%)
  local copies, waits for them, and re-layouts  114 us (21%)
  waiting for transfers between devices  101 us (18%)
    scatter-add x20, other arithmetic, spread(): buffer.at[:, head_atom].add(weighted).at[:, tail_atom].add(-weighted)  141 us
    ppermute x60, starting transfers between devices, with_halo(): after = lax.ppermute(leading, axis, down)  88 us
    ppermute x60, waiting for transfers between devices, with_halo(): before = lax.ppermute(last, axis, up)  80.8 us
    ppermute x60, starting transfers between devices, with_halo(): before = lax.ppermute(last, axis, up)  61.3 us
    gather x8, local copies, waits for them, and re-layouts, couple(): extended[:, head_atom] - extended[:, tail_atom]  32.1 us
    gather x8, local copies, waits for them, and re-layouts, couple(): extended[:, tail_atom]  27.3 us
    ppermute x60, waiting for transfers between devices, with_halo(): after = lax.ppermute(leading, axis, down)  19.9 us
    gather x2, local copies, waits for them, and re-layouts, per_device(): bond_scale = 1.0 / jnp.sqrt(ext_mass[0, head_atom] + ext_mass[0, tail_atom])  12.9 us
  transfers between devices with their start and end apart: 120, of which 103 were waited for; matrix products, arithmetic and copies ran while one was open for 1% of the time, Pallas kernels for 0%

commit v1 on v0

v1 whole, which is shorter than its diff:
```python
import math

import jax
import jax.numpy as jnp
from jax import lax
from jax.experimental import pallas as pl
from jax.experimental.pallas import tpu as pltpu
from jax.sharding import PartitionSpec as P

ORDER = 4
HALO = 192
LANES = 128
NQ = 11
AXES = ("gx", "gy", "gz")
OFFSETS = [(b // 9 - 1, b // 3 % 3 - 1, b % 3 - 1) for b in range(27)]
F32 = jnp.float32
I32 = jnp.int32
SYM = [(0, 0), (1, 1), (2, 2), (0, 1), (0, 2), (1, 2)]


def iota(shape, dim):
    return lax.broadcasted_iota(I32, shape, dim)


def pick(table, index):
    return jnp.take_along_axis(table, index, axis=1, mode="promise_in_bounds")


def spread_row(row, like):
    return jnp.broadcast_to(row, like.shape)


def gather_rows(rows, high, low, base=0):
    result = jnp.zeros(high.shape, rows[0].dtype)
    for r, row in enumerate(rows):
        result = jnp.where(high == base + r, pick(spread_row(row, high), low), result)
    return result


def value_rows(value):
    return [value[r:r + 1, :] for r in range(value.shape[0])]


def gather_value(value, index):
    return gather_rows(value_rows(value), index >> 7, index & 127)


def load_flat(ref, lead, scratch, base, count):
    for r in range(count):
        scratch[base + r:base + r + 1, :] = ref[(*lead, pl.ds(r * LANES, LANES))].reshape(1, LANES)


def axis_sizes(mesh):
    return tuple(mesh.shape[a] for a in AXES)


def my_place():
    return tuple(lax.axis_index(a) for a in AXES)


def one_hot_scatter(values, index, high_rows):
    parts = []
    spots = []
    for r in range(index.shape[0]):
        high = index[r:r + 1, :] >> 7
        low = index[r:r + 1, :] & 127
        hit = jnp.broadcast_to(high, (high_rows, LANES)) == iota((high_rows, LANES), 0)
        parts.append(jnp.concatenate(
            [jnp.where(hit, jnp.broadcast_to(v[r:r + 1, :], (high_rows, LANES)), 0.0) for v in values],
            axis=0).astype(jnp.bfloat16))
        spots.append(jnp.where(
            jnp.broadcast_to(low, (LANES, LANES)) == iota((LANES, LANES), 0), 1.0, 0.0).astype(jnp.bfloat16))
    left = jnp.concatenate(parts, axis=1)
    right = jnp.concatenate(spots, axis=1)
    table = lax.dot_general(left, right, (((1,), (1,)), ((), ())), preferred_element_type=F32)
    return [table[i * high_rows:(i + 1) * high_rows] for i in range(len(values))]


def inverse_tables(index, valid, high_rows):
    where_from = iota(index.shape, 0) * LANES + iota(index.shape, 1)
    spot = jnp.where(valid, index, -1)
    ones = jnp.ones(index.shape, F32)
    upper, lower, count = one_hot_scatter(
        [(where_from >> 5).astype(F32), (where_from & 31).astype(F32), ones], spot, high_rows)
    table = (upper * 32.0 + lower).astype(I32)
    return jnp.where(count > 0.5, table, -1), count


def send_kernel(size, old_ref, move_ref, mass_ref, send_ref, out_ref, table):
    atom_rows = size["atom_rows"]
    send = size["send"]
    pad_rows = size["atom_pad"]
    table[...] = jnp.zeros(table.shape, F32)
    for d in range(3):
        load_flat(old_ref, (d, 0, 0, 0), table, d * pad_rows, atom_rows)
        load_flat(move_ref, (d, 0, 0, 0), table, (3 + d) * pad_rows, atom_rows)
    load_flat(mass_ref, (0, 0, 0), table, 6 * pad_rows, atom_rows)
    lane = iota((pad_rows, LANES), 1)
    index = size["load_send"](send_ref)
    index = jnp.broadcast_to(index, (pad_rows, LANES))
    low = index & 127
    hit = (index >> 7) == iota((pad_rows, LANES), 0)
    message = jnp.zeros((1, LANES), F32)
    for q in range(7):
        got = jnp.where(hit, pick(table[q * pad_rows:(q + 1) * pad_rows, :], low), 0.0)
        row = jnp.sum(got, axis=0, keepdims=True)
        message = jnp.where(lane[0:1] // send == q, row, message)
    for d in range(out_ref.shape[0]):
        out_ref[d, :, :] = message


def chain_sum(value, prev, extra):
    def body(_, carry):
        total, current = carry
        current = gather_value(current, prev)
        return total + current, current

    return lax.fori_loop(0, extra, body, (value, value))[0]


class Local:
    def __init__(self, direction, diag, kappa, tail_mass, following, child, prev, last, extra, many):
        self.e, self.diag, self.kappa, self.tail_mass = direction, diag, kappa, tail_mass
        self.following, self.child, self.prev, self.last = following, child, prev, last
        self.extra, self.many = extra, many

    def total(self, value):
        return chain_sum(value, self.prev, self.extra) if self.many else value

    def apply(self, value):
        result = self.diag * value + self.kappa * gather_value(value, self.following)
        result = result + gather_value(self.total(self.kappa * value), self.child)
        if self.many:
            for d in range(3):
                force = self.e[d] * value
                others = gather_value(self.total(force), self.last) - force
                result = result - jnp.where(self.last >= 0, self.tail_mass * self.e[d] * others, 0.0)
        return result

    def at_head(self, force):
        return force - gather_value(self.total(force), self.child)

    def at_tail(self, force):
        below = gather_value(self.total(force), self.last) if self.many else force
        return gather_value(force, self.following) - below


def both_ways(extra, run):
    @pl.when(extra == 0)
    def _():
        run(False)

    @pl.when(extra > 0)
    def _():
        run(True)


F_NAMES = ["e0", "e1", "e2", "p0", "p1", "p2", "length", "scale", "head_mass", "tail_mass", "diag", "kappa",
           "base1", "g0", "g1", "g2", "g3"]
I_NAMES = ["following", "child", "prev", "last", "root", "slot", "cidx", "extra", "tinv0", "tinv1", "hinv0", "hinv1"]


def f_get(ref, name):
    i = F_NAMES.index(name)
    return ref[8 * i:8 * i + 8, :]


def i_get(ref, name):
    i = I_NAMES.index(name)
    return ref[8 * i:8 * i + 8, :]


def f_put(ref, name, value):
    i = F_NAMES.index(name)
    ref[8 * i:8 * i + 8, :] = value


def i_put(ref, name, value):
    i = I_NAMES.index(name)
    ref[8 * i:8 * i + 8, :] = value


def local_from(state_f, state_i, extra, many):
    return Local([f_get(state_f, f"e{d}") for d in range(3)], f_get(state_f, "diag"), f_get(state_f, "kappa"),
                 f_get(state_f, "tail_mass"), i_get(state_i, "following"), i_get(state_i, "child"),
                 i_get(state_i, "prev"), i_get(state_i, "last"), extra, many)


def compact_rows(values, cidx):
    high = cidx >> 7
    low = cidx & 127
    lane = iota((1, LANES), 1)
    firsts, rests = [], []
    for value in values:
        got = gather_rows(value_rows(value), high, low)
        firsts.append(got[0:1])
        rests.append(got[1:2])
    rows = list(firsts)
    for i in range(0, len(rests), 2):
        other = rests[i + 1] if i + 1 < len(rests) else rests[i]
        rows.append(jnp.where(lane < 64, rests[i], other))
    return rows


def geometry_kernel(size, old_ref, move_ref, mass_ref, head_ref, tail_ref, send_ref, got_ref,
                    state_f, state_i, out_ref, table, remote, rtab, cons):
    X, Y, Z = size["mesh"]
    send = size["send"]
    atom_rows, pad_rows = size["atom_rows"], size["atom_pad"]
    atoms = atom_rows * LANES
    shape = (8, LANES)
    here = iota(shape, 0) * LANES + iota(shape, 1)
    load_flat(head_ref, (0, 0, 0), cons, 0, 8)
    load_flat(tail_ref, (0, 0, 0), cons, 8, 8)
    head = cons[0:8, :]
    tail = cons[8:16, :]
    local = tail < atoms
    for d in range(3):
        load_flat(old_ref, (d, 0, 0, 0), table, d * pad_rows, atom_rows)
        load_flat(move_ref, (d, 0, 0, 0), table, (3 + d) * pad_rows, atom_rows)
    load_flat(mass_ref, (0, 0, 0), table, 6 * pad_rows, atom_rows)
    for d in range(3):
        for r in range(atom_rows):
            a, b = d * pad_rows + r, (3 + d) * pad_rows + r
            table[b:b + 1, :] = table[a:a + 1, :] + table[b:b + 1, :]

    ext_rows = size["ext_rows"]
    tinv, count = inverse_tables(tail, tail >= 0, ext_rows)
    hinv, _ = inverse_tables(head, head >= 0, pad_rows)
    most = jnp.max(jnp.where(iota(count.shape, 0) < atom_rows, count, 0.0))
    extra = jnp.maximum(most.astype(I32) - 1, 0)
    send_row = size["load_send"](send_ref)
    atom_id = iota((pad_rows, LANES), 0) * LANES + iota((pad_rows, LANES), 1)
    for e in range(send):
        which = jnp.broadcast_to(send_row[:, e:e + 1], (pad_rows, LANES))
        hinv = jnp.where(atom_id == which, 8 * LANES + e, hinv)
    cons[16:16 + ext_rows, :] = tinv
    i_put(state_i, "prev", jnp.full(shape, -1, I32))
    i_put(state_i, "last", jnp.where(local, here, -1))

    @pl.when(extra > 0)
    def _():
        def body(c, carry):
            prev, last, inv = carry
            mark = jnp.max(jnp.where(here == c, tail, -1))
            same = tail == mark
            prev = jnp.where(same & (here > c), c, prev)
            last = jnp.where(same & local, c, last)
            spots = iota(inv.shape, 0) * LANES + iota(inv.shape, 1)
            inv = jnp.where(spots == mark, c, inv)
            return prev, last, inv

        prev, last, inv = lax.fori_loop(
            0, 8 * LANES, body, (jnp.full(shape, -1, I32), jnp.full(shape, -1, I32), tinv))
        i_put(state_i, "prev", prev)
        i_put(state_i, "last", last)
        cons[16:16 + ext_rows, :] = inv

    tinv = cons[16:16 + ext_rows, :]
    tail_high, tail_low = tail >> 7, tail & 127
    head_high, head_low = head >> 7, head & 127
    hinv_rows = value_rows(hinv)[:atom_rows]
    following = gather_rows(hinv_rows, tail_high, tail_low)
    following = jnp.where(local, following, -1)
    following = jnp.where(following < 8 * LANES, following, -1)
    child = gather_rows(value_rows(tinv)[:atom_rows], head_high, head_low)
    root = jnp.where(local, -1, tail - atoms)
    slot = root
    for _ in range(3):
        ahead = gather_value(root + 1, following) - 1
        root = jnp.where(root < 0, ahead, root)
    slots = tinv[atom_rows:atom_rows + 4]
    used = slots >= 0
    used_f = jnp.where(used, 1.0, 0.0)
    before = lax.dot_general(
        jnp.concatenate([used_f, jnp.zeros((4, LANES), F32)], axis=0).astype(jnp.bfloat16),
        jnp.where(iota((LANES, LANES), 0) < iota((LANES, LANES), 1), 1.0, 0.0).astype(jnp.bfloat16),
        (((1,), (0,)), ((), ())), preferred_element_type=F32)
    rank_rows = []
    offset = jnp.zeros((1, 1), F32)
    for r in range(4):
        rank_rows.append(before[r:r + 1] + offset)
        offset = offset + jnp.sum(used_f[r:r + 1], axis=1, keepdims=True)
    rank = jnp.concatenate(rank_rows, axis=0)
    number = jnp.where(used, rank, -1.0)
    place = number.astype(I32)
    index4 = jnp.concatenate([place, jnp.where(place >= LANES, place + 64, -1)], axis=0)
    from8 = jnp.concatenate([slots, slots], axis=0)
    upper, lower = one_hot_scatter([(from8 >> 5).astype(F32), (from8 & 31).astype(F32)], index4, 8)
    cidx = (upper * 32.0 + lower).astype(I32)

    gx, gy, gz = my_place()
    for b, (dx, dy, dz) in enumerate(OFFSETS):
        at = (lax.rem(gx + (dx + X), X) * Y + lax.rem(gy + (dy + Y), Y)) * Z + lax.rem(gz + (dz + Z), Z)
        remote[b:b + 1, :] = got_ref[at, :, :]
    sub, lane = iota(shape, 0), iota(shape, 1)
    own = lane // send == sub
    for j in range(4):
        block = remote[8 * j:8 * j + 8, :]
        for q in range(7):
            got = jnp.where(own, pick(block, q * send + lane % send), 0.0)
            row = jnp.sum(got, axis=0, keepdims=True)
            rtab[4 * q + j:4 * q + j + 1, :] = row
    for d in range(3):
        rtab[4 * (3 + d):4 * (3 + d) + 4, :] = rtab[4 * d:4 * d + 4, :] + rtab[4 * (3 + d):4 * (3 + d) + 4, :]

    def rows_of(q):
        return [table[q * pad_rows + r:q * pad_rows + r + 1, :] for r in range(atom_rows)]

    def ext_rows_of(q):
        return rows_of(q) + [rtab[4 * q + j:4 * q + j + 1, :] for j in range(4)]

    head_at = [gather_rows(rows_of(q), head_high, head_low) for q in range(7)]
    tail_at = [gather_rows(ext_rows_of(q), tail_high, tail_low) for q in range(7)]
    bond = [head_at[d] - tail_at[d] for d in range(3)]
    gap = [head_at[3 + d] - tail_at[3 + d] for d in range(3)]
    length = jnp.maximum(jnp.sqrt(bond[0] * bond[0] + bond[1] * bond[1] + bond[2] * bond[2]), 0.5)
    direction = [bond[d] / length for d in range(3)]
    scale = 1.0 / jnp.sqrt(head_at[6] + tail_at[6])
    force = [scale * direction[d] for d in range(3)]
    head_mass = head_at[6]
    tail_mass = jnp.where(local, tail_at[6], 0.0)
    norm = force[0] * force[0] + force[1] * force[1] + force[2] * force[2]
    diag = 1.0 - norm * (head_mass + tail_mass)
    ahead = [gather_value(force[d], following) for d in range(3)]
    kappa = tail_mass * (force[0] * ahead[0] + force[1] * ahead[1] + force[2] * ahead[2])
    right = scale * ((direction[0] * gap[0] + direction[1] * gap[1] + direction[2] * gap[2]) - length)
    for d in range(3):
        f_put(state_f, f"e{d}", force[d])
        f_put(state_f, f"p{d}", gap[d])
    f_put(state_f, "length", length)
    f_put(state_f, "scale", scale)
    f_put(state_f, "head_mass", head_mass)
    f_put(state_f, "tail_mass", tail_mass)
    f_put(state_f, "diag", diag)
    f_put(state_f, "kappa", kappa)
    i_put(state_i, "following", following)
    i_put(state_i, "child", child)
    i_put(state_i, "root", root)
    i_put(state_i, "slot", slot)
    i_put(state_i, "cidx", cidx)
    i_put(state_i, "extra", jnp.broadcast_to(extra, shape))
    i_put(state_i, "tinv0", tinv[0:8])
    i_put(state_i, "tinv1", tinv[8:16])
    i_put(state_i, "hinv0", hinv[0:8])
    i_put(state_i, "hinv1", hinv[8:16])

    def run(many):
        operator = local_from(state_f, state_i, extra, many)
        terms = [right]
        unit = [jnp.where(local, 0.0, 1.0)]
        for k in range(ORDER):
            terms.append(operator.apply(terms[-1]))
            if k < ORDER - 1:
                unit.append(operator.apply(unit[-1]))
        base = terms[0]
        for term in terms[1:]:
            base = base + term
        f_put(state_f, "base1", base)
        summed = unit[0]
        f_put(state_f, "g0", summed)
        for k in range(1, ORDER):
            summed = summed + unit[k]
            f_put(state_f, f"g{k}", summed)
        rows = compact_rows(force + unit[1:] + terms, cidx)
        rows = rows + value_rows(number)
        for r, row in enumerate(rows):
            out_ref[0, r, :, :] = row

    both_ways(extra, run)
    for d in range(1, out_ref.shape[0]):
        for r in range(size["rows2"]):
            out_ref[d, r, :, :] = out_ref[0, r, :, :]


def lane_fields(tile):
    lane = iota((1, LANES), 1)
    return lane


def block_masks(tile, send, rows):
    per = LANES // send
    block = iota((rows, LANES), 1) // send + per * tile
    return block // 9 - 1, block // 3 % 3 - 1, block % 3 - 1, [b for b in range(per * tile, per * tile + per)]


def choose(options, field, values):
    result = options[values[0]]
    for v in values[1:]:
        result = jnp.where(field == v, options[v], result)
    return result


def expand_dense(size, load_row, number_rows, slots, dense):
    X, Y, Z = size["mesh"]
    R = Y * Z
    nq = len(slots)
    for x in range(X):
        for l in range(4):
            number = load_row(number_rows, x, l)
            high = number >> 7
            low = number & 127
            for i, q in enumerate(slots):
                first, rest, half = q
                a = pick(load_row("q", x, first), low)
                b = pick(load_row("q", x, rest), (low & 63) + 64 * half)
                value = jnp.where(number < 0, 0.0, jnp.where(high == 0, a, b))
                dense[x, i, :, l * LANES:(l + 1) * LANES] = value


def aligned(size, dense, q, target, tile):
    X, Y, Z = size["mesh"]
    send = size["send"]
    R = Y * Z
    dx, dy, dz, blocks = block_masks(tile, send, R)
    blocks = [b for b in blocks if b < 27]
    span = pl.ds(tile * LANES, LANES)
    offs = [sorted({OFFSETS[b][k] for b in blocks}) for k in range(3)]
    value = choose({o: dense[lax.rem(target + (X - o), X), q, :, span] for o in offs[0]}, dx, offs[0])
    row_z = iota((R, LANES), 0) % Z
    options = {0: value}
    if 1 in offs[2]:
        options[1] = jnp.where(row_z == 0, turn(value, Z - 1, R), turn(value, -1, R))
    if -1 in offs[2]:
        options[-1] = jnp.where(row_z == Z - 1, turn(value, -(Z - 1), R), turn(value, 1, R))
    value = choose(options, dz, offs[2])
    value = choose({o: turn(value, -o * Z, R) for o in offs[1]}, dy, offs[1])
    return value


def turn(value, by, rows):
    shift = (-by) % rows
    return value if shift == 0 else pltpu.roll(value, shift, 0)


def lane_total(parts, send):
    total = parts[0]
    for part in parts[1:]:
        total = total + part
    step = LANES // 2
    while step >= send:
        total = total + pltpu.roll(total, step, 1)
        step //= 2
    return total


def times(matrix, vector):
    full = {}
    for i, (a, b) in enumerate(SYM):
        full[a, b] = full[b, a] = matrix[i]
    return [full[a, 0] * vector[0] + full[a, 1] * vector[1] + full[a, 2] * vector[2] for a in range(3)]


def recurrence(first, matrices, mass):
    sums, scaled = [], []
    for k in range(ORDER + 1):
        value = first[k]
        for j in range(k):
            back = times(matrices[k - 1 - j], scaled[j])
            value = [value[d] - back[d] for d in range(3)]
        sums.append(value)
        scaled.append([mass * value[d] for d in range(3)])
    total = sums[0]
    for value in sums[1:]:
        total = [total[d] + value[d] for d in range(3)]
    return scaled, total, [mass * total[d] for d in range(3)]


def own_rows(size, place, tiles, tile):
    X, Y, Z = size["mesh"]
    R = Y * Z
    gx, gy, gz = place
    dx, dy, dz, blocks = block_masks(tile, size["send"], R)
    blocks = [b for b in blocks if b < 27]
    wanted = lax.rem(gy + dy + Y, Y) * Z + lax.rem(gz + dz + Z, Z)
    offs = sorted({OFFSETS[b][0] for b in blocks})
    value = choose({o: tiles[o + 1] for o in offs}, dx, offs)
    return jnp.sum(jnp.where(wanted == iota((R, LANES), 0), value, 0.0), axis=0, keepdims=True)


def strided(ref, first, rows, stride):
    if rows <= 8:
        return ref[pl.ds(first, rows, stride=stride), :]
    return jnp.concatenate(
        [ref[pl.ds(first + 8 * i * stride, 8, stride=stride), :] for i in range(rows // 8)], axis=0)


def middle_kernel(size, state_f, state_i, got1, got2, out_ref, pair_ref, force_ref, matrix_ref, keep_ref, dense):
    X, Y, Z = size["mesh"]
    send = size["send"]
    R = Y * Z
    rows2 = size["rows2"]
    place = my_place()
    gx, gy, gz = place

    def load_row(kind, x, r):
        row = strided(got2, x * R * rows2 + (size["map_row"] + r if kind == "map" else r), R, rows2)
        return row.astype(I32) if kind == "map" else row

    expand_dense(size, load_row, "map", [(q, NQ + q // 2, q % 2) for q in range(NQ)], dense)
    scaled_tiles, total_tiles, own_total = [], [], None
    for t in range(3):
        target = lax.rem(gx + (t - 1 + X), X)
        sums = {}
        for tile in range(4):
            q = [aligned(size, dense, i, target, tile) for i in range(NQ)]
            force, unit, terms = q[0:3], q[3:6], q[6:11]
            for d in range(3):
                force_ref[t, d, :, tile * LANES:(tile + 1) * LANES] = force[d]
                for k in range(ORDER + 1):
                    sums.setdefault(("v", k, d), []).append(force[d] * terms[k])
            for s, (a, b) in enumerate(SYM):
                square = force[a] * force[b]
                sums.setdefault(("b", 0, s), []).append(square)
                for k in range(3):
                    sums.setdefault(("b", k + 1, s), []).append(square * unit[k])
        sums = {key: lane_total(parts, send) for key, parts in sums.items()}
        mass = pick(strided(got1, target * R, R, 1), 6 * send + iota((R, LANES), 1) % send)
        matrices = [[sums["b", k, s] for s in range(6)] for k in range(ORDER)]
        for k in range(ORDER):
            for s in range(6):
                matrix_ref[t, 6 * k + s, :, :] = matrices[k][s]
        matrix_ref[t, 24, :, :] = mass
        scaled, total, full = recurrence(
            [[sums["v", k, d] for d in range(3)] for k in range(ORDER + 1)], matrices, mass)
        scaled_tiles.append(scaled)
        total_tiles.append(full)
        if t == 1:
            own_total = total
    me = gy * Z + gz
    keep_ref[...] = jnp.zeros(keep_ref.shape, F32)
    mine = iota((R, LANES), 0) == me
    for d in range(3):
        keep_ref[d:d + 1, :] = jnp.sum(jnp.where(mine, own_total[d], 0.0), axis=0, keepdims=True)
    corrections = [[] for _ in range(ORDER)]
    moves = [[] for _ in range(3)]
    for tile in range(4):
        force = []
        for d in range(3):
            value = dense[gx, d, :, tile * LANES:(tile + 1) * LANES]
            row = jnp.sum(jnp.where(mine, value, 0.0), axis=0, keepdims=True)
            keep_ref[8 + 4 * d + tile:9 + 4 * d + tile, :] = row
            force.append(row)
        for j in range(ORDER):
            rows = [own_rows(size, place, [scaled_tiles[t][j][d] for t in range(3)], tile) for d in range(3)]
            corrections[j].append(force[0] * rows[0] + force[1] * rows[1] + force[2] * rows[2])
        for d in range(3):
            moves[d].append(own_rows(size, place, [total_tiles[t][d] for t in range(3)], tile))
    root = i_get(state_i, "root")
    slot = i_get(state_i, "slot")
    solved = f_get(state_f, "base1")
    for j in range(ORDER):
        at = gather_rows(corrections[j], root >> 7, root & 127)
        solved = solved - f_get(state_f, f"g{ORDER - 1 - j}") * at
    moved = [gather_rows(moves[d], slot >> 7, slot & 127) for d in range(3)]
    extra = jnp.max(i_get(state_i, "extra"))
    cidx = i_get(state_i, "cidx")

    def run(many):
        operator = local_from(state_f, state_i, extra, many)
        local = slot < 0
        stretch = []
        for d in range(3):
            force = operator.e[d] * solved
            change = f_get(state_f, "head_mass") * operator.at_head(force)
            other = jnp.where(local, operator.tail_mass * operator.at_tail(force), -moved[d])
            stretch.append(f_get(state_f, f"p{d}") - (change - other))
        length = f_get(state_f, "length")
        current = stretch[0] * stretch[0] + stretch[1] * stretch[1] + stretch[2] * stretch[2]
        target = jnp.sqrt(jnp.maximum(2.0 * length * length - current, 0.5 * length * length))
        terms = [f_get(state_f, "scale") * (length - target)]
        for _ in range(ORDER):
            terms.append(operator.apply(terms[-1]))
        base = terms[0]
        for term in terms[1:]:
            base = base + term
        pair_ref[0:8, :] = solved
        pair_ref[8:16, :] = base
        rows = compact_rows(terms, cidx)
        for r, row in enumerate(rows):
            out_ref[0, r:r + 1, :] = row

    both_ways(extra, run)
    for d in range(1, out_ref.shape[0]):
        out_ref[d, :, :] = out_ref[0, :, :]


def final_kernel(size, old_ref, move_ref, mass_ref, state_f, state_i, got2, got3, pair_ref, force_ref, matrix_ref,
                 keep_ref, pos_ref, mult_ref, dense):
    X, Y, Z = size["mesh"]
    send = size["send"]
    R = Y * Z
    rows2 = size["rows2"]
    place = my_place()
    gx, gy, gz = place

    def load_row(kind, x, r):
        if kind == "map":
            return strided(got2, x * R * rows2 + size["map_row"] + r, R, rows2).astype(I32)
        return strided(got3, x * R * 8 + r, R, 8)

    nk = ORDER + 1
    expand_dense(size, load_row, "map", [(q, nk + q // 2, q % 2) for q in range(nk)], dense)
    scaled_tiles, own_total = [], None
    for t in range(3):
        target = lax.rem(gx + (t - 1 + X), X)
        sums = {}
        for tile in range(4):
            terms = [aligned(size, dense, i, target, tile) for i in range(nk)]
            for d in range(3):
                force = force_ref[t, d, :, tile * LANES:(tile + 1) * LANES]
                for k in range(nk):
                    sums.setdefault((k, d), []).append(force * terms[k])
        sums = {key: lane_total(parts, send) for key, parts in sums.items()}
        matrices = [[matrix_ref[t, 6 * k + s, :, :] for s in range(6)] for k in range(ORDER)]
        scaled, total, _ = recurrence(
            [[sums[k, d] for d in range(3)] for k in range(nk)], matrices, matrix_ref[t, 24, :, :])
        scaled_tiles.append(scaled)
        if t == 1:
            own_total = total
    mine = iota((R, LANES), 0) == gy * Z + gz
    corrections = [[] for _ in range(ORDER)]
    for tile in range(4):
        force = [keep_ref[8 + 4 * d + tile:9 + 4 * d + tile, :] for d in range(3)]
        for j in range(ORDER):
            rows = [own_rows(size, place, [scaled_tiles[t][j][d] for t in range(3)], tile) for d in range(3)]
            corrections[j].append(force[0] * rows[0] + force[1] * rows[1] + force[2] * rows[2])
    root = i_get(state_i, "root")
    solved = pair_ref[8:16, :]
    for j in range(ORDER):
        at = gather_rows(corrections[j], root >> 7, root & 127)
        solved = solved - f_get(state_f, f"g{ORDER - 1 - j}") * at
    both = pair_ref[0:8, :] + solved
    for r in range(8):
        mult_ref[0, 0, 0, pl.ds(r * LANES, LANES)] = both[r, :]
    extra = jnp.max(i_get(state_i, "extra"))

    def run(many):
        operator = local_from(state_f, state_i, extra, many)
        for d in range(3):
            force = operator.e[d] * both
            below = value_rows(operator.total(force))
            sent = keep_ref[d:d + 1, :] + jnp.sum(jnp.where(mine, own_total[d], 0.0), axis=0, keepdims=True)
            above = value_rows(force) + [-sent]
            for part, count in enumerate(size["atom_parts"]):
                hinv = i_get(state_i, f"hinv{part}")
                tinv = i_get(state_i, f"tinv{part}")
                change = gather_rows(above, hinv >> 7, hinv & 127) - gather_rows(below, tinv >> 7, tinv & 127)
                for r in range(count):
                    span = pl.ds((8 * part + r) * LANES, LANES)
                    start = old_ref[d, 0, 0, 0, span] + move_ref[d, 0, 0, 0, span]
                    pos_ref[d, 0, 0, 0, span] = start - mass_ref[0, 0, 0, span] * change[r, :]

    both_ways(extra, run)


def share(message):
    return lax.all_to_all(message, AXES, split_axis=0, concat_axis=0, tiled=True)


def make_per_device(mesh):
    sizes = axis_sizes(mesh)
    X, Y, Z = sizes
    devices = X * Y * Z
    R = Y * Z

    def per_device(old_pos, displacement, inv_mass, bond_head, bond_tail, send_list):
        atoms = old_pos.shape[-1]
        bonds = bond_head.shape[-1]
        send = send_list.shape[-1]
        atom_rows = atoms // LANES
        assert atoms % LANES == 0 and bonds == 8 * LANES and LANES % send == 0 and atom_rows <= 16
        rows2 = NQ + (NQ + 1) // 2 + 4

        def load_send(ref):
            one = ref[0, 0, 0:1, :]
            return jnp.concatenate([one] * (LANES // send), axis=1)

        size = dict(mesh=sizes, send=send, atom_rows=atom_rows, atom_pad=16, ext_rows=16, rows2=rows2,
                    map_row=NQ + (NQ + 1) // 2, load_send=load_send,
                    atom_parts=[min(8, atom_rows), max(atom_rows - 8, 0)])

        def call(kernel, outs, scratch, *args):
            def wrapped(*refs):
                kernel(size, *refs)

            return pl.pallas_call(
                wrapped, out_shape=outs, scratch_shapes=scratch,
                in_specs=[pl.BlockSpec(memory_space=pltpu.VMEM)] * len(args),
                out_specs=jax.tree.map(lambda _: pl.BlockSpec(memory_space=pltpu.VMEM), outs),
                compiler_params=pltpu.CompilerParams(vmem_limit_bytes=32 * 1024 * 1024),
            )(*args)

        S = jax.ShapeDtypeStruct
        one = call(send_kernel, S((devices, 1, LANES), F32), [pltpu.VMEM((7 * 16, LANES), F32)],
                   old_pos, displacement, inv_mass, send_list)
        got1 = share(one)
        state_f, state_i, two = call(
            geometry_kernel,
            (S((8 * len(F_NAMES), LANES), F32), S((8 * len(I_NAMES), LANES), I32), S((devices, rows2, 1, LANES), F32)),
            [pltpu.VMEM((7 * 16, LANES), F32), pltpu.VMEM((32, LANES), F32), pltpu.VMEM((32, LANES), F32),
             pltpu.VMEM((32, LANES), I32)],
            old_pos, displacement, inv_mass, bond_head, bond_tail, send_list, got1)
        got2 = share(two).reshape(devices * rows2, LANES)
        wide = 4 * LANES
        three, pair, force, matrix, keep = call(
            middle_kernel,
            (S((devices, 8, LANES), F32), S((16, LANES), F32), S((3, 3, R, wide), F32), S((3, 25, R, LANES), F32),
             S((24, LANES), F32)),
            [pltpu.VMEM((X, NQ, R, wide), F32)],
            state_f, state_i, got1.reshape(devices, LANES), got2)
        got3 = share(three).reshape(devices * 8, LANES)
        return call(
            final_kernel,
            (S(old_pos.shape, F32), S(bond_head.shape, F32)),
            [pltpu.VMEM((X, ORDER + 1, R, wide), F32)],
            old_pos, displacement, inv_mass, state_f, state_i, got2, got3, pair, force, matrix, keep)

    return per_device


def solution(mesh):
    return jax.shard_map(
        make_per_device(mesh),
        mesh=mesh,
        in_specs=(
            P(None, "gx", "gy", "gz", None),
            P(None, "gx", "gy", "gz", None),
            P("gx", "gy", "gz", None),
            P("gx", "gy", "gz", None),
            P("gx", "gy", "gz", None),
            P("gx", "gy", "gz", None),
        ),
        out_specs=(P(None, "gx", "gy", "gz", None), P("gx", "gy", "gz", None)),
        check_vma=False,
    )
```

time: 549 us -> 54.6 us (0.10); the launches traced: 541 us -> 54.2 us
  other arithmetic: 173 us -> 0 us
  starting transfers between devices: 149 us -> 0 us
  local copies, waits for them, and re-layouts: 114 us -> 2.8 us
  waiting for transfers between devices: 101 us -> 0 us
  blocking collectives: 0 us -> 38.8 us
  Pallas kernels: 0 us -> 11.9 us
    scatter-add x30 -> x0, other arithmetic: 152 us -> none  [the longest x20 141 us: spread(): buffer.at[:, head_atom].add(weighted).at[:, tail_atom].add(-weighted)]
    ppermute x120 -> x0, starting transfers between devices: 149 us -> none  [the longest x60 88 us: with_halo(): after = lax.ppermute(leading, axis, down)]
    gather x46 -> x0, local copies, waits for them, and re-layouts: 102 us -> none  [the longest x8 32.1 us: couple(): extended[:, head_atom] - extended[:, tail_atom]]
    ppermute x120 -> x0, waiting for transfers between devices: 101 us -> none  [the longest x60 80.8 us: with_halo(): before = lax.ppermute(last, axis, up)]
    all_to_all x0 -> x3, blocking collectives: none -> 38.8 us  [share(): lax.all_to_all(message, AXES, split_axis=0, concat_axis=0, tiled=True)]
    pallas_call x0 -> x4, Pallas kernels: none -> 11.9 us  [call(): pl.pallas_call(wrapped, out_shape=outs, scratch_shapes=scratch, in_specs=...]
    reduce_sum x21 -> x0, other arithmetic: 9.59 us -> none  [the longest x8 7.33 us: couple(): jnp.sum(direction * (extended[:, head_atom] - extended[:, tail_atom]), ax...]
    concatenate x65 -> x0, other arithmetic: 6.08 us -> none  [the longest x8 4.37 us: couple(): jnp.concatenate([shift_vec, remote.reshape(3, wide_count)], axis=1)]
  transfers between devices with their start and end apart: 120 -> 0, of which waited for: 103 -> 0; matrix products, arithmetic and copies ran while one was open for 1% -> 0% of each run, Pallas kernels for 0% -> 0%
where the time goes in v1:
time: 54.6 us; the launch traced here: 54.2 us
  blocking collectives  38.8 us (71%)
  Pallas kernels  11.9 us (22%)
  local copies, waits for them, and re-layouts  2.8 us (5%)
  between operations  0.69 us (1%)
    all_to_all x3, blocking collectives, share(): lax.all_to_all(message, AXES, split_axis=0, concat_axis=0, tiled=True)  38.8 us
    pallas_call x4, Pallas kernels, call(): pl.pallas_call(wrapped, out_shape=outs, scratch_shapes=scratch, in_specs=...  11.9 us
    unnamed x14, local copies, waits for them, and re-layouts  2.8 us

profile of v1, /device:TPU:0, one launch (start us, length us, event | category | flops | bytes accessed | tf_op | source)
XLA Modules:
  0.0 54.2 jit_solution(10737631522117370102)
XLA Ops:
  0.6 0.0 copy-start
  0.6 0.7 %copy-done = f32[3,1,1,1,1536]{4,3,2,1,0:T(1,128)S(1)} copy-done((f32[3,1,1,1,1536]{4,3,2,1,0:T(1,128)S(1)}, f32[3,1,1,1,1536]{4,3,2,1,0:T(1,128)}, u32[]{:S(2)}) %copy-start) | copy-done | bytes 18456
  1.4 0.0 copy-start.2
  1.4 0.7 %copy-done.2 = f32[3,1,1,1,1536]{4,3,2,1,0:T(1,128)S(1)} copy-done((f32[3,1,1,1,1536]{4,3,2,1,0:T(1,128)S(1)}, f32[3,1,1,1,1536]{4,3,2,1,0:T(1,128)}, u32[]{:S(2)}) %copy-start.2) | copy-done | bytes 18456
  2.1 0.0 copy-start.3
  2.1 0.7 %copy-done.3 = f32[1,1,1,1536]{3,2,1,0:T(1,128)S(1)} copy-done((f32[1,1,1,1536]{3,2,1,0:T(1,128)S(1)}, f32[1,1,1,1536]{3,2,1,0:T(1,128)}, u32[]{:S(2)}) %copy-start.3) | copy-done | bytes 6168
  2.8 0.0 copy-start.6
  2.8 0.7 %copy-done.6 = s32[1,1,1,16]{3,2,1,0:T(1,128)S(1)} copy-done((s32[1,1,1,16]{3,2,1,0:T(1,128)S(1)}, s32[1,1,1,16]{3,2,1,0:T(1,128)}, u32[]{:S(2)}) %copy-start.6) | copy-done | bytes 88
  3.4 0.2 shard_map.77
  3.6 0.0 copy-start.4
  3.6 0.0 copy-start.5
  3.6 14.3 %all_to_all.15.refs_6_ = f32[32,1,128]{2,1,0:T(1,128)S(1)} all-to-all(f32[32,1,128]{2,1,0:T(1,128)S(1)} %shard_map.77), channel_id=1, replica_groups=mesh['gx'=4,'gy'=2,'gz'=4] {'gx','gy','gz'}, dimensions={0} | all-to-all | bytes 32768 | tf_op jit(solution)/shard_map/all_to_all | solution.py:658
  18.0 0.0 copy-done.4
  18.0 0.0 copy-done.5
  18.0 1.8 %shard_map.78 = (f32[136,128]{1,0:T(8,128)S(1)}, s32[96,128]{1,0:T(8,128)S(1)}, f32[32,21,1,128]{3,2,1,0:T(1,128)S(1)}) custom-call(f32[3,1,1,1,1536]{4,3,2,1,0:T(1,128)S(1)} %copy-done, f32[3,1,1,1,1536]{4,3,2,1,0:T(1,128)S(1)} %copy-done.2, f32[1,1,1,1536]{3,2,1,0:T(1,128)S(1)} %copy-done.3, s32[1,1,1,1024]{3,2,1,0:T(1,128)S(1)} %copy-done.4, ...), custom_call_target="tpu_custom_call" | custom-call | tf_op jit(solution)/shard_map/pallas_call | solution.py:687
  19.8 13.0 %all_to_all.16 = f32[32,21,1,128]{3,2,1,0:T(1,128)S(1)} all-to-all(f32[32,21,1,128]{3,2,1,0:T(1,128)S(1)} %get-tuple-element.12), channel_id=1, replica_groups=mesh['gx'=4,'gy'=2,'gz'=4] {'gx','gy','gz'}, dimensions={0} | all-to-all | bytes 688128 | tf_op jit(solution)/shard_map/all_to_all | solution.py:658
  32.8 8.2 %shard_map.79 = (f32[32,8,128]{2,1,0:T(8,128)S(1)}, f32[16,128]{1,0:T(8,128)S(1)}, f32[3,3,8,512]{3,2,1,0:T(8,128)S(1)}, f32[3,25,8,128]{3,2,1,0:T(8,128)S(1)}, f32[24,128]{1,0:T(8,128)S(1)}) custom-call(f32[136,128]{1,0:T(8,128)S(1)} %get-tuple-element.10.refs_0_.refs_3_, s32[96,128]{1,0:T(8,128)S(1)} %get-tuple-element.11.refs_1_.refs_4_, ...), custom_call_target="tpu_custom_call" | custom-call | tf_op jit(solution)/shard_map/pallas_call | solution.py:687
  40.9 0.0 copy-start.1
  41.0 11.5 %all_to_all.17 = f32[32,8,128]{2,1,0:T(8,128)S(1)} all-to-all(f32[32,8,128]{2,1,0:T(8,128)S(1)} %get-tuple-element.13), channel_id=1, replica_groups=mesh['gx'=4,'gy'=2,'gz'=4] {'gx','gy','gz'}, dimensions={0} | all-to-all | bytes 262144 | tf_op jit(solution)/shard_map/all_to_all | solution.py:658
  52.4 0.0 copy-done.1
  52.5 1.7 %shard_map.80 = (f32[3,1,1,1,1536]{4,3,2,1,0:T(1,128)}, f32[1,1,1,1024]{3,2,1,0:T(1,128)}) custom-call(f32[3,1,1,1,1536]{4,3,2,1,0:T(1,128)S(1)} %copy-done.1, f32[3,1,1,1,1536]{4,3,2,1,0:T(1,128)S(1)} %copy-done.2, f32[1,1,1,1536]{3,2,1,0:T(1,128)S(1)} %copy-done.3, f32[136,128]{1,0:T(8,128)S(1)} %get-tuple-element.10.refs_0_.refs_3_, ...), custom_call_target="tpu_custom_call" | custom-call | tf_op jit(solution)/shard_map/pallas_call | solution.py:687
Async XLA Ops:
  0.6 0.7 %copy-start = (f32[3,1,1,1,1536]{4,3,2,1,0:T(1,128)S(1)}, f32[3,1,1,1,1536]{4,3,2,1,0:T(1,128)}, u32[]{:S(2)}) copy-start(f32[3,1,1,1,1536]{4,3,2,1,0:T(1,128)} %refs_0_.5) | copy-start | bytes 55300
  1.4 0.7 %copy-start.2 = (f32[3,1,1,1,1536]{4,3,2,1,0:T(1,128)S(1)}, f32[3,1,1,1,1536]{4,3,2,1,0:T(1,128)}, u32[]{:S(2)}) copy-start(f32[3,1,1,1,1536]{4,3,2,1,0:T(1,128)} %refs_1_.5) | copy-start | bytes 55300
  2.1 0.7 %copy-start.3 = (f32[1,1,1,1536]{3,2,1,0:T(1,128)S(1)}, f32[1,1,1,1536]{3,2,1,0:T(1,128)}, u32[]{:S(2)}) copy-start(f32[1,1,1,1536]{3,2,1,0:T(1,128)} %refs_2_.5) | copy-start | bytes 18436
  2.8 0.7 %copy-start.6 = (s32[1,1,1,16]{3,2,1,0:T(1,128)S(1)}, s32[1,1,1,16]{3,2,1,0:T(1,128)}, u32[]{:S(2)}) copy-start(s32[1,1,1,16]{3,2,1,0:T(1,128)} %refs_5_.1) | copy-start | bytes 196
  3.6 14.4 %copy-start.4 = (s32[1,1,1,1024]{3,2,1,0:T(1,128)S(1)}, s32[1,1,1,1024]{3,2,1,0:T(1,128)}, u32[]{:S(2)}) copy-start(s32[1,1,1,1024]{3,2,1,0:T(1,128)} %refs_3_.3) | copy-start | bytes 12292
  3.6 14.4 %copy-start.5 = (s32[1,1,1,1024]{3,2,1,0:T(1,128)S(1)}, s32[1,1,1,1024]{3,2,1,0:T(1,128)}, u32[]{:S(2)}) copy-start(s32[1,1,1,1024]{3,2,1,0:T(1,128)} %refs_4_.1) | copy-start | bytes 12292
  40.9 11.5 %copy-start.1 = (f32[3,1,1,1,1536]{4,3,2,1,0:T(1,128)S(1)}, f32[3,1,1,1,1536]{4,3,2,1,0:T(1,128)}, u32[]{:S(2)}) copy-start(f32[3,1,1,1,1536]{4,3,2,1,0:T(1,128)} %refs_0_.5) | copy-start | bytes 55300

commit v2 on v1

--- a/solution.py
+++ b/solution.py
@@ -86,18 +86,33 @@
     return jnp.where(count > 0.5, table, -1), count
 
 
-def send_kernel(size, old_ref, move_ref, mass_ref, send_ref, out_ref, table):
+def send_kernel(size, old_hbm, move_hbm, mass_hbm, head_hbm, tail_hbm, send_hbm, out_ref, table, cons,
+                old_ref, move_ref, mass_ref, head_ref, tail_ref, send_ref, sems):
     atom_rows = size["atom_rows"]
     send = size["send"]
     pad_rows = size["atom_pad"]
+    copies = [pltpu.make_async_copy(src, dst, sems.at[i]) for i, (src, dst) in enumerate(
+        [(old_hbm, old_ref), (move_hbm, move_ref), (mass_hbm, mass_ref), (send_hbm, send_ref), (head_hbm, head_ref),
+         (tail_hbm, tail_ref)])]
+    for copy in copies:
+        copy.start()
+    for copy in copies:
+        copy.wait()
     table[...] = jnp.zeros(table.shape, F32)
-    for d in range(3):
-        load_flat(old_ref, (d, 0, 0, 0), table, d * pad_rows, atom_rows)
-        load_flat(move_ref, (d, 0, 0, 0), table, (3 + d) * pad_rows, atom_rows)
+    for r in range(atom_rows):
+        span = pl.ds(r * LANES, LANES)
+        for d in range(3):
+            old = old_ref[d, 0, 0, 0, span].reshape(1, LANES)
+            a, b = d * pad_rows + r, (3 + d) * pad_rows + r
+            table[a:a + 1, :] = old
+            table[b:b + 1, :] = old + move_ref[d, 0, 0, 0, span].reshape(1, LANES)
     load_flat(mass_ref, (0, 0, 0), table, 6 * pad_rows, atom_rows)
+    load_flat(head_ref, (0, 0, 0), cons, 0, 8)
+    load_flat(tail_ref, (0, 0, 0), cons, 8, 8)
     lane = iota((pad_rows, LANES), 1)
-    index = size["load_send"](send_ref)
-    index = jnp.broadcast_to(index, (pad_rows, LANES))
+    send_row = size["load_send"](send_ref)
+    cons[16:24, :] = jnp.broadcast_to(send_row, (8, LANES))
+    index = jnp.broadcast_to(send_row, (pad_rows, LANES))
     low = index & 127
     hit = (index >> 7) == iota((pad_rows, LANES), 0)
     message = jnp.zeros((1, LANES), F32)
@@ -202,39 +217,27 @@
     return rows
 
 
-def geometry_kernel(size, old_ref, move_ref, mass_ref, head_ref, tail_ref, send_ref, got_ref,
-                    state_f, state_i, out_ref, table, remote, rtab, cons):
-    X, Y, Z = size["mesh"]
+def map_kernel(size, table, cons, state_i, number_ref, head_ref, tail_ref, work):
+    atom_rows, pad_rows = size["atom_rows"], size["atom_pad"]
     send = size["send"]
-    atom_rows, pad_rows = size["atom_rows"], size["atom_pad"]
     atoms = atom_rows * LANES
     shape = (8, LANES)
     here = iota(shape, 0) * LANES + iota(shape, 1)
-    load_flat(head_ref, (0, 0, 0), cons, 0, 8)
-    load_flat(tail_ref, (0, 0, 0), cons, 8, 8)
     head = cons[0:8, :]
     tail = cons[8:16, :]
     local = tail < atoms
-    for d in range(3):
-        load_flat(old_ref, (d, 0, 0, 0), table, d * pad_rows, atom_rows)
-        load_flat(move_ref, (d, 0, 0, 0), table, (3 + d) * pad_rows, atom_rows)
-    load_flat(mass_ref, (0, 0, 0), table, 6 * pad_rows, atom_rows)
-    for d in range(3):
-        for r in range(atom_rows):
-            a, b = d * pad_rows + r, (3 + d) * pad_rows + r
-            table[b:b + 1, :] = table[a:a + 1, :] + table[b:b + 1, :]
 
     ext_rows = size["ext_rows"]
     tinv, count = inverse_tables(tail, tail >= 0, ext_rows)
     hinv, _ = inverse_tables(head, head >= 0, pad_rows)
     most = jnp.max(jnp.where(iota(count.shape, 0) < atom_rows, count, 0.0))
     extra = jnp.maximum(most.astype(I32) - 1, 0)
-    send_row = size["load_send"](send_ref)
+    send_row = cons[16:17, :]
     atom_id = iota((pad_rows, LANES), 0) * LANES + iota((pad_rows, LANES), 1)
     for e in range(send):
         which = jnp.broadcast_to(send_row[:, e:e + 1], (pad_rows, LANES))
         hinv = jnp.where(atom_id == which, 8 * LANES + e, hinv)
-    cons[16:16 + ext_rows, :] = tinv
+    work[0:ext_rows, :] = tinv
     i_put(state_i, "prev", jnp.full(shape, -1, I32))
     i_put(state_i, "last", jnp.where(local, here, -1))
 
@@ -254,9 +257,9 @@
             0, 8 * LANES, body, (jnp.full(shape, -1, I32), jnp.full(shape, -1, I32), tinv))
         i_put(state_i, "prev", prev)
         i_put(state_i, "last", last)
-        cons[16:16 + ext_rows, :] = inv
-
-    tinv = cons[16:16 + ext_rows, :]
+        work[0:ext_rows, :] = inv
+
+    tinv = work[0:ext_rows, :]
     tail_high, tail_low = tail >> 7, tail & 127
     head_high, head_low = head >> 7, head & 127
     hinv_rows = value_rows(hinv)[:atom_rows]
@@ -289,6 +292,36 @@
     upper, lower = one_hot_scatter([(from8 >> 5).astype(F32), (from8 & 31).astype(F32)], index4, 8)
     cidx = (upper * 32.0 + lower).astype(I32)
 
+    number_ref[0:4, :] = number
+    number_ref[4:8, :] = number
+    i_put(state_i, "following", following)
+    i_put(state_i, "child", child)
+    i_put(state_i, "root", root)
+    i_put(state_i, "slot", slot)
+    i_put(state_i, "cidx", cidx)
+    i_put(state_i, "extra", jnp.broadcast_to(extra, shape))
+    i_put(state_i, "tinv0", tinv[0:8])
+    i_put(state_i, "tinv1", tinv[8:16])
+    i_put(state_i, "hinv0", hinv[0:8])
+    i_put(state_i, "hinv1", hinv[8:16])
+
+    def rows_of(q):
+        return [table[q * pad_rows + r:q * pad_rows + r + 1, :] for r in range(atom_rows)]
+
+    for q in range(7):
+        head_ref[8 * q:8 * q + 8, :] = gather_rows(rows_of(q), head_high, head_low)
+        tail_ref[8 * q:8 * q + 8, :] = gather_rows(rows_of(q), tail_high, tail_low)
+
+
+def geometry_kernel(size, state_i, number_ref, head_ref, tail_ref, got_ref, state_f, out_ref, remote, rtab):
+    X, Y, Z = size["mesh"]
+    send = size["send"]
+    shape = (8, LANES)
+    slot = i_get(state_i, "slot")
+    local = slot < 0
+    following = i_get(state_i, "following")
+    cidx = i_get(state_i, "cidx")
+    extra = jnp.max(i_get(state_i, "extra"))
     gx, gy, gz = my_place()
     for b, (dx, dy, dz) in enumerate(OFFSETS):
         at = (lax.rem(gx + (dx + X), X) * Y + lax.rem(gy + (dy + Y), Y)) * Z + lax.rem(gz + (dz + Z), Z)
@@ -301,17 +334,12 @@
             got = jnp.where(own, pick(block, q * send + lane % send), 0.0)
             row = jnp.sum(got, axis=0, keepdims=True)
             rtab[4 * q + j:4 * q + j + 1, :] = row
-    for d in range(3):
-        rtab[4 * (3 + d):4 * (3 + d) + 4, :] = rtab[4 * d:4 * d + 4, :] + rtab[4 * (3 + d):4 * (3 + d) + 4, :]
-
-    def rows_of(q):
-        return [table[q * pad_rows + r:q * pad_rows + r + 1, :] for r in range(atom_rows)]
-
-    def ext_rows_of(q):
-        return rows_of(q) + [rtab[4 * q + j:4 * q + j + 1, :] for j in range(4)]
-
-    head_at = [gather_rows(rows_of(q), head_high, head_low) for q in range(7)]
-    tail_at = [gather_rows(ext_rows_of(q), tail_high, tail_low) for q in range(7)]
+    slot_high, slot_low = slot >> 7, slot & 127
+    head_at = [head_ref[8 * q:8 * q + 8, :] for q in range(7)]
+    tail_at = []
+    for q in range(7):
+        afar = gather_rows([rtab[4 * q + j:4 * q + j + 1, :] for j in range(4)], slot_high, slot_low)
+        tail_at.append(jnp.where(local, tail_ref[8 * q:8 * q + 8, :], afar))
     bond = [head_at[d] - tail_at[d] for d in range(3)]
     gap = [head_at[3 + d] - tail_at[3 + d] for d in range(3)]
     length = jnp.maximum(jnp.sqrt(bond[0] * bond[0] + bond[1] * bond[1] + bond[2] * bond[2]), 0.5)
@@ -334,17 +362,6 @@
     f_put(state_f, "tail_mass", tail_mass)
     f_put(state_f, "diag", diag)
     f_put(state_f, "kappa", kappa)
-    i_put(state_i, "following", following)
-    i_put(state_i, "child", child)
-    i_put(state_i, "root", root)
-    i_put(state_i, "slot", slot)
-    i_put(state_i, "cidx", cidx)
-    i_put(state_i, "extra", jnp.broadcast_to(extra, shape))
-    i_put(state_i, "tinv0", tinv[0:8])
-    i_put(state_i, "tinv1", tinv[8:16])
-    i_put(state_i, "hinv0", hinv[0:8])
-    i_put(state_i, "hinv1", hinv[8:16])
-
     def run(many):
         operator = local_from(state_f, state_i, extra, many)
         terms = [right]
@@ -363,7 +380,7 @@
             summed = summed + unit[k]
             f_put(state_f, f"g{k}", summed)
         rows = compact_rows(force + unit[1:] + terms, cidx)
-        rows = rows + value_rows(number)
+        rows = rows + value_rows(number_ref[0:4, :])
         for r, row in enumerate(rows):
             out_ref[0, r, :, :] = row
 
@@ -433,15 +450,18 @@
     return value if shift == 0 else pltpu.roll(value, shift, 0)
 
 
-def lane_total(parts, send):
-    total = parts[0]
-    for part in parts[1:]:
-        total = total + part
-    step = LANES // 2
-    while step >= send:
-        total = total + pltpu.roll(total, step, 1)
-        step //= 2
-    return total
+def lane_totals(sums, send):
+    stack = jnp.concatenate([parts[0] + parts[1] + parts[2] + parts[3] for parts in sums.values()], axis=0)
+    pieces = []
+    for _ in range(3):
+        piece = stack.astype(jnp.bfloat16)
+        pieces.append(piece)
+        stack = stack - piece.astype(F32)
+    same = iota((3 * LANES, LANES), 0) % send == iota((3 * LANES, LANES), 1) % send
+    table = jnp.dot(jnp.concatenate(pieces, axis=1), jnp.where(same, 1.0, 0.0).astype(jnp.bfloat16),
+                    preferred_element_type=F32)
+    rows = table.shape[0] // len(sums)
+    return {key: table[i * rows:(i + 1) * rows] for i, key in enumerate(sums)}
 
 
 def times(matrix, vector):
@@ -514,7 +534,7 @@
                 sums.setdefault(("b", 0, s), []).append(square)
                 for k in range(3):
                     sums.setdefault(("b", k + 1, s), []).append(square * unit[k])
-        sums = {key: lane_total(parts, send) for key, parts in sums.items()}
+        sums = lane_totals(sums, send)
         mass = pick(strided(got1, target * R, R, 1), 6 * send + iota((R, LANES), 1) % send)
         matrices = [[sums["b", k, s] for s in range(6)] for k in range(ORDER)]
         for k in range(ORDER):
@@ -585,7 +605,7 @@
         out_ref[d, :, :] = out_ref[0, :, :]
 
 
-def final_kernel(size, old_ref, move_ref, mass_ref, state_f, state_i, got2, got3, pair_ref, force_ref, matrix_ref,
+def final_kernel(size, table, state_f, state_i, got2, got3, pair_ref, force_ref, matrix_ref,
                  keep_ref, pos_ref, mult_ref, dense):
     X, Y, Z = size["mesh"]
     send = size["send"]
@@ -611,7 +631,7 @@
                 force = force_ref[t, d, :, tile * LANES:(tile + 1) * LANES]
                 for k in range(nk):
                     sums.setdefault((k, d), []).append(force * terms[k])
-        sums = {key: lane_total(parts, send) for key, parts in sums.items()}
+        sums = lane_totals(sums, send)
         matrices = [[matrix_ref[t, 6 * k + s, :, :] for s in range(6)] for k in range(ORDER)]
         scaled, total, _ = recurrence(
             [[sums[k, d] for d in range(3)] for k in range(nk)], matrices, matrix_ref[t, 24, :, :])
@@ -648,8 +668,9 @@
                 change = gather_rows(above, hinv >> 7, hinv & 127) - gather_rows(below, tinv >> 7, tinv & 127)
                 for r in range(count):
                     span = pl.ds((8 * part + r) * LANES, LANES)
-                    start = old_ref[d, 0, 0, 0, span] + move_ref[d, 0, 0, 0, span]
-                    pos_ref[d, 0, 0, 0, span] = start - mass_ref[0, 0, 0, span] * change[r, :]
+                    at = 8 * part + r
+                    pos_ref[d, 0, 0, 0, span] = (table[(3 + d) * size["atom_pad"] + at, :]
+                                                 - table[6 * size["atom_pad"] + at, :] * change[r, :])
 
     both_ways(extra, run)
 
@@ -680,27 +701,34 @@
                     map_row=NQ + (NQ + 1) // 2, load_send=load_send,
                     atom_parts=[min(8, atom_rows), max(atom_rows - 8, 0)])
 
-        def call(kernel, outs, scratch, *args):
+        def call(kernel, outs, scratch, *args, space=pltpu.VMEM):
             def wrapped(*refs):
                 kernel(size, *refs)
 
             return pl.pallas_call(
                 wrapped, out_shape=outs, scratch_shapes=scratch,
-                in_specs=[pl.BlockSpec(memory_space=pltpu.VMEM)] * len(args),
+                in_specs=[pl.BlockSpec(memory_space=space)] * len(args),
                 out_specs=jax.tree.map(lambda _: pl.BlockSpec(memory_space=pltpu.VMEM), outs),
                 compiler_params=pltpu.CompilerParams(vmem_limit_bytes=32 * 1024 * 1024),
-            )(*args)
+            )(*[pltpu.with_memory_space_constraint(a, space) for a in args] if space == pltpu.HBM else args)
 
         S = jax.ShapeDtypeStruct
-        one = call(send_kernel, S((devices, 1, LANES), F32), [pltpu.VMEM((7 * 16, LANES), F32)],
-                   old_pos, displacement, inv_mass, send_list)
+        one, table, cons = call(
+            send_kernel, (S((devices, 1, LANES), F32), S((7 * 16, LANES), F32), S((24, LANES), I32)),
+            [pltpu.VMEM(old_pos.shape, F32), pltpu.VMEM(old_pos.shape, F32), pltpu.VMEM(inv_mass.shape, F32),
+             pltpu.VMEM(bond_head.shape, I32), pltpu.VMEM(bond_tail.shape, I32), pltpu.VMEM(send_list.shape, I32),
+             pltpu.SemaphoreType.DMA((6,))],
+            old_pos, displacement, inv_mass, bond_head, bond_tail, send_list, space=pltpu.HBM)
         got1 = share(one)
-        state_f, state_i, two = call(
+        state_i, number, head_at, tail_at = call(
+            map_kernel,
+            (S((8 * len(I_NAMES), LANES), I32), S((8, LANES), F32), S((56, LANES), F32), S((56, LANES), F32)),
+            [pltpu.VMEM((16, LANES), I32)], table, cons)
+        state_f, two = call(
             geometry_kernel,
-            (S((8 * len(F_NAMES), LANES), F32), S((8 * len(I_NAMES), LANES), I32), S((devices, rows2, 1, LANES), F32)),
-            [pltpu.VMEM((7 * 16, LANES), F32), pltpu.VMEM((32, LANES), F32), pltpu.VMEM((32, LANES), F32),
-             pltpu.VMEM((32, LANES), I32)],
-            old_pos, displacement, inv_mass, bond_head, bond_tail, send_list, got1)
+            (S((8 * len(F_NAMES), LANES), F32), S((devices, rows2, 1, LANES), F32)),
+            [pltpu.VMEM((32, LANES), F32), pltpu.VMEM((32, LANES), F32)],
+            state_i, number, head_at, tail_at, got1)
         got2 = share(two).reshape(devices * rows2, LANES)
         wide = 4 * LANES
         three, pair, force, matrix, keep = call(
@@ -714,7 +742,7 @@
             final_kernel,
             (S(old_pos.shape, F32), S(bond_head.shape, F32)),
             [pltpu.VMEM((X, ORDER + 1, R, wide), F32)],
-            old_pos, displacement, inv_mass, state_f, state_i, got2, got3, pair, force, matrix, keep)
+            table, state_f, state_i, got2, got3, pair, force, matrix, keep)
 
     return per_device
 

time: 54.6 us -> 46.4 us (0.85)
  blocking collectives: 38.8 us -> 24.5 us
  starting transfers between devices: 0 us -> 7.33 us
  waiting for transfers between devices: 0 us -> 6.23 us
  Pallas kernels: 11.9 us -> 7.47 us
  local copies, waits for them, and re-layouts: 2.8 us -> 0 us
    all_to_all x3 -> x2, blocking collectives: 38.8 us -> 24.5 us  [share(): lax.all_to_all(message, AXES, split_axis=0, concat_axis=0, tiled=True)]
    all_to_all x0 -> x1, starting transfers between devices: none -> 7.33 us  [share(): lax.all_to_all(message, AXES, split_axis=0, concat_axis=0, tiled=True)]
    all_to_all x0 -> x1, waiting for transfers between devices: none -> 6.23 us  [share(): lax.all_to_all(message, AXES, split_axis=0, concat_axis=0, tiled=True)]
    pallas_call x4 -> x5, Pallas kernels: 11.9 us -> 7.47 us  [call(): pl.pallas_call(wrapped, out_shape=outs, scratch_shapes=scratch, in_specs=...]
    unnamed x14 -> x0, local copies, waits for them, and re-layouts: 2.8 us -> none
  transfers between devices with their start and end apart: 0 -> 1, of which waited for: 0 -> 1; matrix products, arithmetic and copies ran while one was open for 0% -> 0% of each run, Pallas kernels for 0% -> 2%
where the time goes in v2:
time: 46.4 us; the launch traced here: 46.2 us
  blocking collectives  24.5 us (53%)
  Pallas kernels  7.47 us (16%)
  starting transfers between devices  7.33 us (16%)
  waiting for transfers between devices  6.23 us (13%)
  between operations  0.66 us (1%)
    all_to_all x2, blocking collectives, share(): lax.all_to_all(message, AXES, split_axis=0, concat_axis=0, tiled=True)  24.5 us
    pallas_call x5, Pallas kernels, call(): pl.pallas_call(wrapped, out_shape=outs, scratch_shapes=scratch, in_specs=...  7.47 us
    all_to_all x1, starting transfers between devices, share(): lax.all_to_all(message, AXES, split_axis=0, concat_axis=0, tiled=True)  7.33 us
    all_to_all x1, waiting for transfers between devices, share(): lax.all_to_all(message, AXES, split_axis=0, concat_axis=0, tiled=True)  6.23 us
  transfers between devices with their start and end apart: 1, of which 1 were waited for; matrix products, arithmetic and copies ran while one was open for 0% of the time, Pallas kernels for 2%

profile of v2, /device:TPU:0, one launch (start us, length us, event | category | flops | bytes accessed | tf_op | source)
XLA Modules:
  0.0 46.2 jit_solution(880753699490976838)
XLA Ops:
  0.6 1.6 %shard_map.77 = (f32[32,1,128]{2,1,0:T(1,128)}, f32[112,128]{1,0:T(8,128)S(1)}, s32[24,128]{1,0:T(8,128)S(1)}) custom-call(f32[3,1,1,1,1536]{4,3,2,1,0:T(1,128)} %refs_0_.1, f32[3,1,1,1,1536]{4,3,2,1,0:T(1,128)} %refs_1_.1, f32[1,1,1,1536]{3,2,1,0:T(1,128)} %refs_2_.1, s32[1,1,1,1024]{3,2,1,0:T(1,128)} %refs_3_.1, s32[1,1,1,1024]{3,2,1,0:T(1,128)} %refs_4_.1, ...), custom_call_target="tpu_custom_call" | custom-call | tf_op jit(solution)/shard_map/pallas_call | solution.py:708
  2.2 7.3 %all-to-all-start = ((f32[32,1,128]{2,1,0:T(1,128)}), f32[32,1,128]{2,1,0:T(1,128)S(1)}, u32[]{:S(2)}, u32[]{:S(2)}) async-start(f32[32,1,128]{2,1,0:T(1,128)} %get-tuple-element.22), calls=%async_computation | async-start | bytes 32768 | tf_op jit(solution)/shard_map/all_to_all | solution.py:679
  9.6 0.9 %shard_map.78 = (s32[96,128]{1,0:T(8,128)S(1)}, f32[8,128]{1,0:T(8,128)S(1)}, f32[56,128]{1,0:T(8,128)S(1)}, f32[56,128]{1,0:T(8,128)S(1)}) custom-call(f32[112,128]{1,0:T(8,128)S(1)} %get-tuple-element.16.refs_0_, s32[24,128]{1,0:T(8,128)S(1)} %get-tuple-element.17.refs_1_), custom_call_target="tpu_custom_call" | custom-call | tf_op jit(solution)/shard_map/pallas_call | solution.py:708
  10.5 6.2 %all-to-all-done.refs_4_ = f32[32,1,128]{2,1,0:T(1,128)S(1)} async-done(((f32[32,1,128]{2,1,0:T(1,128)}), f32[32,1,128]{2,1,0:T(1,128)S(1)}, u32[]{:S(2)}, u32[]{:S(2)}) %all-to-all-start) | async-done | bytes 16416 | tf_op jit(solution)/shard_map/all_to_all | solution.py:679
  16.7 1.1 %shard_map.79 = (f32[136,128]{1,0:T(8,128)S(1)}, f32[32,21,1,128]{3,2,1,0:T(1,128)S(1)}) custom-call(s32[96,128]{1,0:T(8,128)S(1)} %get-tuple-element.18.refs_0_.refs_1_.refs_2_, f32[8,128]{1,0:T(8,128)S(1)} %get-tuple-element.19.refs_1_, f32[56,128]{1,0:T(8,128)S(1)} %get-tuple-element.20.refs_2_, f32[56,128]{1,0:T(8,128)S(1)} %get-tuple-element.21.refs_3_, ...), custom_call_target="tpu_custom_call" | custom-call | tf_op jit(solution)/shard_map/pallas_call | solution.py:708
  17.8 13.0 %all_to_all.15 = f32[32,21,1,128]{3,2,1,0:T(1,128)S(1)} all-to-all(f32[32,21,1,128]{3,2,1,0:T(1,128)S(1)} %get-tuple-element.24), channel_id=1, replica_groups=mesh['gx'=4,'gy'=2,'gz'=4] {'gx','gy','gz'}, dimensions={0} | all-to-all | bytes 688128 | tf_op jit(solution)/shard_map/all_to_all | solution.py:679
  30.8 2.1 %shard_map.80 = (f32[32,8,128]{2,1,0:T(8,128)S(1)}, f32[16,128]{1,0:T(8,128)S(1)}, f32[3,3,8,512]{3,2,1,0:T(8,128)S(1)}, f32[3,25,8,128]{3,2,1,0:T(8,128)S(1)}, f32[24,128]{1,0:T(8,128)S(1)}) custom-call(f32[136,128]{1,0:T(8,128)S(1)} %get-tuple-element.23.refs_0_.refs_1_, s32[96,128]{1,0:T(8,128)S(1)} %get-tuple-element.18.refs_0_.refs_1_.refs_2_, ...), custom_call_target="tpu_custom_call" | custom-call | tf_op jit(solution)/shard_map/pallas_call | solution.py:708
  32.9 11.5 %all_to_all.16 = f32[32,8,128]{2,1,0:T(8,128)S(1)} all-to-all(f32[32,8,128]{2,1,0:T(8,128)S(1)} %get-tuple-element.25), channel_id=1, replica_groups=mesh['gx'=4,'gy'=2,'gz'=4] {'gx','gy','gz'}, dimensions={0} | all-to-all | bytes 262144 | tf_op jit(solution)/shard_map/all_to_all | solution.py:679
  44.4 1.7 %shard_map.81 = (f32[3,1,1,1,1536]{4,3,2,1,0:T(1,128)}, f32[1,1,1,1024]{3,2,1,0:T(1,128)}) custom-call(f32[112,128]{1,0:T(8,128)S(1)} %get-tuple-element.16.refs_0_, f32[136,128]{1,0:T(8,128)S(1)} %get-tuple-element.23.refs_0_.refs_1_, s32[96,128]{1,0:T(8,128)S(1)} %get-tuple-element.18.refs_0_.refs_1_.refs_2_, f32[672,128]{1,0:T(8,128)S(1)} %bitcast.4, ...), custom_call_target="tpu_custom_call" | custom-call | tf_op jit(solution)/shard_map/pallas_call | solution.py:708
Async XLA Ops:
  2.2 14.5 %all-to-all-start = ((f32[32,1,128]{2,1,0:T(1,128)}), f32[32,1,128]{2,1,0:T(1,128)S(1)}, u32[]{:S(2)}, u32[]{:S(2)}) async-start(f32[32,1,128]{2,1,0:T(1,128)} %get-tuple-element.22), calls=%async_computation | async-start | bytes 32768 | tf_op jit(solution)/shard_map/all_to_all | solution.py:679

commit v3 on v2

--- a/solution.py
+++ b/solution.py
@@ -492,7 +492,7 @@
     gx, gy, gz = place
     dx, dy, dz, blocks = block_masks(tile, size["send"], R)
     blocks = [b for b in blocks if b < 27]
-    wanted = lax.rem(gy + dy + Y, Y) * Z + lax.rem(gz + dz + Z, Z)
+    wanted = lax.rem(dy + Y, Y) * Z + lax.rem(gz + dz + Z, Z)
     offs = sorted({OFFSETS[b][0] for b in blocks})
     value = choose({o: tiles[o + 1] for o in offs}, dx, offs)
     return jnp.sum(jnp.where(wanted == iota((R, LANES), 0), value, 0.0), axis=0, keepdims=True)
@@ -505,7 +505,20 @@
         [ref[pl.ds(first + 8 * i * stride, 8, stride=stride), :] for i in range(rows // 8)], axis=0)
 
 
-def middle_kernel(size, state_f, state_i, got1, got2, out_ref, pair_ref, force_ref, matrix_ref, keep_ref, dense):
+def plane(size, refs, x, row, stride):
+    Y, Z = size["mesh"][1:]
+    gy = lax.axis_index("gy")
+    pieces = []
+    for k in range(Y):
+        if len(refs) > 1:
+            pieces.append(strided(refs[k], x * Z * stride + row, Z, stride))
+        else:
+            pieces.append(strided(refs[0], (x * Y + lax.rem(gy + k, Y)) * Z * stride + row, Z, stride))
+    return jnp.concatenate(pieces, axis=0)
+
+
+def middle_kernel(size, state_f, state_i, got1, *refs):
+    *got2, out_ref, pair_ref, force_ref, matrix_ref, keep_ref, dense = refs
     X, Y, Z = size["mesh"]
     send = size["send"]
     R = Y * Z
@@ -514,7 +527,7 @@
     gx, gy, gz = place
 
     def load_row(kind, x, r):
-        row = strided(got2, x * R * rows2 + (size["map_row"] + r if kind == "map" else r), R, rows2)
+        row = plane(size, got2, x, size["map_row"] + r if kind == "map" else r, rows2)
         return row.astype(I32) if kind == "map" else row
 
     expand_dense(size, load_row, "map", [(q, NQ + q // 2, q % 2) for q in range(NQ)], dense)
@@ -535,7 +548,7 @@
                 for k in range(3):
                     sums.setdefault(("b", k + 1, s), []).append(square * unit[k])
         sums = lane_totals(sums, send)
-        mass = pick(strided(got1, target * R, R, 1), 6 * send + iota((R, LANES), 1) % send)
+        mass = pick(plane(size, [got1], target, 0, 1), 6 * send + iota((R, LANES), 1) % send)
         matrices = [[sums["b", k, s] for s in range(6)] for k in range(ORDER)]
         for k in range(ORDER):
             for s in range(6):
@@ -547,9 +560,8 @@
         total_tiles.append(full)
         if t == 1:
             own_total = total
-    me = gy * Z + gz
     keep_ref[...] = jnp.zeros(keep_ref.shape, F32)
-    mine = iota((R, LANES), 0) == me
+    mine = iota((R, LANES), 0) == gz
     for d in range(3):
         keep_ref[d:d + 1, :] = jnp.sum(jnp.where(mine, own_total[d], 0.0), axis=0, keepdims=True)
     corrections = [[] for _ in range(ORDER)]
@@ -605,8 +617,8 @@
         out_ref[d, :, :] = out_ref[0, :, :]
 
 
-def final_kernel(size, table, state_f, state_i, got2, got3, pair_ref, force_ref, matrix_ref,
-                 keep_ref, pos_ref, mult_ref, dense):
+def final_kernel(size, table, state_f, state_i, got3, pair_ref, force_ref, matrix_ref, keep_ref, *refs):
+    *got2, pos_ref, mult_ref, dense = refs
     X, Y, Z = size["mesh"]
     send = size["send"]
     R = Y * Z
@@ -616,8 +628,8 @@
 
     def load_row(kind, x, r):
         if kind == "map":
-            return strided(got2, x * R * rows2 + size["map_row"] + r, R, rows2).astype(I32)
-        return strided(got3, x * R * 8 + r, R, 8)
+            return plane(size, got2, x, size["map_row"] + r, rows2).astype(I32)
+        return plane(size, [got3], x, r, 8)
 
     nk = ORDER + 1
     expand_dense(size, load_row, "map", [(q, nk + q // 2, q % 2) for q in range(nk)], dense)
@@ -638,7 +650,7 @@
         scaled_tiles.append(scaled)
         if t == 1:
             own_total = total
-    mine = iota((R, LANES), 0) == gy * Z + gz
+    mine = iota((R, LANES), 0) == gz
     corrections = [[] for _ in range(ORDER)]
     for tile in range(4):
         force = [keep_ref[8 + 4 * d + tile:9 + 4 * d + tile, :] for d in range(3)]
@@ -675,8 +687,8 @@
     both_ways(extra, run)
 
 
-def share(message):
-    return lax.all_to_all(message, AXES, split_axis=0, concat_axis=0, tiled=True)
+def share(message, axes=AXES):
+    return lax.all_to_all(message, axes, split_axis=0, concat_axis=0, tiled=True)
 
 
 def make_per_device(mesh):
@@ -726,23 +738,25 @@
             [pltpu.VMEM((16, LANES), I32)], table, cons)
         state_f, two = call(
             geometry_kernel,
-            (S((8 * len(F_NAMES), LANES), F32), S((devices, rows2, 1, LANES), F32)),
+            (S((8 * len(F_NAMES), LANES), F32), S((X * Z, rows2, 1, LANES), F32)),
             [pltpu.VMEM((32, LANES), F32), pltpu.VMEM((32, LANES), F32)],
             state_i, number, head_at, tail_at, got1)
-        got2 = share(two).reshape(devices * rows2, LANES)
+        got2 = share(two, ("gx", "gz"))
+        got2 = [got2] + [lax.ppermute(got2, "gy", [((i + k) % Y, i) for i in range(Y)]) for k in range(1, Y)]
+        got2 = [g.reshape(X * Z * rows2, LANES) for g in got2]
         wide = 4 * LANES
         three, pair, force, matrix, keep = call(
             middle_kernel,
             (S((devices, 8, LANES), F32), S((16, LANES), F32), S((3, 3, R, wide), F32), S((3, 25, R, LANES), F32),
              S((24, LANES), F32)),
             [pltpu.VMEM((X, NQ, R, wide), F32)],
-            state_f, state_i, got1.reshape(devices, LANES), got2)
+            state_f, state_i, got1.reshape(devices, LANES), *got2)
         got3 = share(three).reshape(devices * 8, LANES)
         return call(
             final_kernel,
             (S(old_pos.shape, F32), S(bond_head.shape, F32)),
             [pltpu.VMEM((X, ORDER + 1, R, wide), F32)],
-            table, state_f, state_i, got2, got3, pair, force, matrix, keep)
+            table, state_f, state_i, got3, pair, force, matrix, keep, *got2)
 
     return per_device
 

time: 46.4 us -> 44.8 us (0.966)
  blocking collectives: 24.5 us -> 21.5 us
  waiting for transfers between devices: 6.23 us -> 7.63 us
    all_to_all x2, blocking collectives: 24.5 us -> 21.5 us  [share(): lax.all_to_all(message, axes, split_axis=0, concat_axis=0, tiled=True)]
    ppermute x0 -> x1, waiting for transfers between devices: none -> 1.4 us  [per_device(): lax.ppermute(got2, 'gy', [((i + k) % Y, i) for i in range(Y)])]
  transfers between devices with their start and end apart: 1 -> 2, of which waited for: 1 -> 2; matrix products, arithmetic and copies ran while one was open for 0% -> 0% of each run, Pallas kernels for 2% -> 2%
where the time goes in v3:
time: 44.8 us; the launch traced here: 44.5 us
  blocking collectives  21.5 us (48%)
  waiting for transfers between devices  7.63 us (17%)
  Pallas kernels  7.38 us (16%)
  starting transfers between devices  7.33 us (16%)
  between operations  0.66 us (1%)
    all_to_all x2, blocking collectives, share(): lax.all_to_all(message, axes, split_axis=0, concat_axis=0, tiled=True)  21.5 us
    pallas_call x5, Pallas kernels, call(): pl.pallas_call(wrapped, out_shape=outs, scratch_shapes=scratch, in_specs=...  7.38 us
    all_to_all x1, starting transfers between devices, share(): lax.all_to_all(message, axes, split_axis=0, concat_axis=0, tiled=True)  7.33 us
    all_to_all x1, waiting for transfers between devices, share(): lax.all_to_all(message, axes, split_axis=0, concat_axis=0, tiled=True)  6.23 us
    ppermute x1, waiting for transfers between devices, per_device(): lax.ppermute(got2, 'gy', [((i + k) % Y, i) for i in range(Y)])  1.4 us
  transfers between devices with their start and end apart: 2, of which 2 were waited for; matrix products, arithmetic and copies ran while one was open for 0% of the time, Pallas kernels for 2%

profile of v3, /device:TPU:0, one launch (start us, length us, event | category | flops | bytes accessed | tf_op | source)
XLA Modules:
  0.0 44.5 jit_solution(9319316107270098900)
XLA Ops:
  0.6 1.6 %shard_map.77 = (f32[32,1,128]{2,1,0:T(1,128)}, f32[112,128]{1,0:T(8,128)S(1)}, s32[24,128]{1,0:T(8,128)S(1)}) custom-call(f32[3,1,1,1,1536]{4,3,2,1,0:T(1,128)} %refs_0_.1, f32[3,1,1,1,1536]{4,3,2,1,0:T(1,128)} %refs_1_.1, f32[1,1,1,1536]{3,2,1,0:T(1,128)} %refs_2_.1, s32[1,1,1,1024]{3,2,1,0:T(1,128)} %refs_3_.1, s32[1,1,1,1024]{3,2,1,0:T(1,128)} %refs_4_.1, ...), custom_call_target="tpu_custom_call" | custom-call | tf_op jit(solution)/shard_map/pallas_call | solution.py:720
  2.2 7.3 %all-to-all-start = ((f32[32,1,128]{2,1,0:T(1,128)}), f32[32,1,128]{2,1,0:T(1,128)S(1)}, u32[]{:S(2)}, u32[]{:S(2)}) async-start(f32[32,1,128]{2,1,0:T(1,128)} %get-tuple-element.22), calls=%async_computation | async-start | bytes 32768 | tf_op jit(solution)/shard_map/all_to_all | solution.py:691
  9.6 0.9 %shard_map.78 = (s32[96,128]{1,0:T(8,128)S(1)}, f32[8,128]{1,0:T(8,128)S(1)}, f32[56,128]{1,0:T(8,128)S(1)}, f32[56,128]{1,0:T(8,128)S(1)}) custom-call(f32[112,128]{1,0:T(8,128)S(1)} %get-tuple-element.16.refs_0_, s32[24,128]{1,0:T(8,128)S(1)} %get-tuple-element.17.refs_1_), custom_call_target="tpu_custom_call" | custom-call | tf_op jit(solution)/shard_map/pallas_call | solution.py:720
  10.5 6.2 %all-to-all-done.refs_4_ = f32[32,1,128]{2,1,0:T(1,128)S(1)} async-done(((f32[32,1,128]{2,1,0:T(1,128)}), f32[32,1,128]{2,1,0:T(1,128)S(1)}, u32[]{:S(2)}, u32[]{:S(2)}) %all-to-all-start) | async-done | bytes 16416 | tf_op jit(solution)/shard_map/all_to_all | solution.py:691
  16.7 1.0 %shard_map.79 = (f32[136,128]{1,0:T(8,128)S(1)}, f32[16,21,1,128]{3,2,1,0:T(1,128)S(1)}) custom-call(s32[96,128]{1,0:T(8,128)S(1)} %get-tuple-element.18.refs_0_.refs_1_.refs_2_, f32[8,128]{1,0:T(8,128)S(1)} %get-tuple-element.19.refs_1_, f32[56,128]{1,0:T(8,128)S(1)} %get-tuple-element.20.refs_2_, f32[56,128]{1,0:T(8,128)S(1)} %get-tuple-element.21.refs_3_, ...), custom_call_target="tpu_custom_call" | custom-call | tf_op jit(solution)/shard_map/pallas_call | solution.py:720
  17.7 11.4 %all_to_all.15 = f32[16,21,1,128]{3,2,1,0:T(1,128)S(1)} all-to-all(f32[16,21,1,128]{3,2,1,0:T(1,128)S(1)} %get-tuple-element.24), channel_id=1, replica_groups=mesh['gx'=4,'gy'=2,'gz'=4] {'gx','gz'}, dimensions={0} | all-to-all | bytes 344064 | tf_op jit(solution)/shard_map/all_to_all | solution.py:691
  29.1 0.0 collective-permute-start
  29.1 1.4 %collective-permute-done = f32[16,21,1,128]{3,2,1,0:T(1,128)S(1)} collective-permute-done((f32[16,21,1,128]{3,2,1,0:T(1,128)S(1)}, f32[16,21,1,128]{3,2,1,0:T(1,128)S(1)}, u32[]{:S(2)}, u32[]{:S(2)}) %collective-permute-start) | collective-permute-done | bytes 172064 | tf_op jit(solution)/shard_map/ppermute | solution.py:745
  30.6 2.1 %shard_map.80 = (f32[32,8,128]{2,1,0:T(8,128)S(1)}, f32[16,128]{1,0:T(8,128)S(1)}, f32[3,3,8,512]{3,2,1,0:T(8,128)S(1)}, f32[3,25,8,128]{3,2,1,0:T(8,128)S(1)}, f32[24,128]{1,0:T(8,128)S(1)}) custom-call(f32[136,128]{1,0:T(8,128)S(1)} %get-tuple-element.23.refs_0_.refs_1_, s32[96,128]{1,0:T(8,128)S(1)} %get-tuple-element.18.refs_0_.refs_1_.refs_2_, ...), custom_call_target="tpu_custom_call" | custom-call | tf_op jit(solution)/shard_map/pallas_call | solution.py:720
  32.7 10.1 %all_to_all.16 = f32[32,8,128]{2,1,0:T(8,128)S(1)} all-to-all(f32[32,8,128]{2,1,0:T(8,128)S(1)} %get-tuple-element.25), channel_id=1, replica_groups=mesh['gx'=4,'gy'=2,'gz'=4] {'gx','gy','gz'}, dimensions={0} | all-to-all | bytes 262144 | tf_op jit(solution)/shard_map/all_to_all | solution.py:691
  42.8 1.7 %shard_map.81 = (f32[3,1,1,1,1536]{4,3,2,1,0:T(1,128)}, f32[1,1,1,1024]{3,2,1,0:T(1,128)}) custom-call(f32[112,128]{1,0:T(8,128)S(1)} %get-tuple-element.16.refs_0_, f32[136,128]{1,0:T(8,128)S(1)} %get-tuple-element.23.refs_0_.refs_1_, s32[96,128]{1,0:T(8,128)S(1)} %get-tuple-element.18.refs_0_.refs_1_.refs_2_, f32[256,128]{1,0:T(8,128)S(1)} %bitcast.8, ...), custom_call_target="tpu_custom_call" | custom-call | tf_op jit(solution)/shard_map/pallas_call | solution.py:720
Async XLA Ops:
  2.2 14.5 %all-to-all-start = ((f32[32,1,128]{2,1,0:T(1,128)}), f32[32,1,128]{2,1,0:T(1,128)S(1)}, u32[]{:S(2)}, u32[]{:S(2)}) async-start(f32[32,1,128]{2,1,0:T(1,128)} %get-tuple-element.22), calls=%async_computation | async-start | bytes 32768 | tf_op jit(solution)/shard_map/all_to_all | solution.py:691
  29.1 1.4 %collective-permute-start = (f32[16,21,1,128]{3,2,1,0:T(1,128)S(1)}, f32[16,21,1,128]{3,2,1,0:T(1,128)S(1)}, u32[]{:S(2)}, u32[]{:S(2)}) collective-permute-start(f32[16,21,1,128]{3,2,1,0:T(1,128)S(1)} %all_to_all.15), channel_id=1, source_target_pairs={{4,0},{0,4},{5,1},{1,5},{6,2},{2,6},{7,3},{3,7},{12,8},{8,12},{13,... | collective-permute-start | bytes 516104 | tf_op jit(solution)/shard_map/ppermute | solution.py:745

commit v4 on v3

--- a/solution.py
+++ b/solution.py
@@ -206,9 +206,9 @@
     low = cidx & 127
     lane = iota((1, LANES), 1)
     firsts, rests = [], []
-    for value in values:
+    for i, value in enumerate(values):
         got = gather_rows(value_rows(value), high, low)
-        firsts.append(got[0:1])
+        firsts.append(got[2:3] if i % 2 else got[0:1])
         rests.append(got[1:2])
     rows = list(firsts)
     for i in range(0, len(rests), 2):
@@ -280,9 +280,11 @@
         jnp.where(iota((LANES, LANES), 0) < iota((LANES, LANES), 1), 1.0, 0.0).astype(jnp.bfloat16),
         (((1,), (0,)), ((), ())), preferred_element_type=F32)
     rank_rows = []
+    starts = []
     offset = jnp.zeros((1, 1), F32)
     for r in range(4):
         rank_rows.append(before[r:r + 1] + offset)
+        starts.append(offset)
         offset = offset + jnp.sum(used_f[r:r + 1], axis=1, keepdims=True)
     rank = jnp.concatenate(rank_rows, axis=0)
     number = jnp.where(used, rank, -1.0)
@@ -291,7 +293,13 @@
     from8 = jnp.concatenate([slots, slots], axis=0)
     upper, lower = one_hot_scatter([(from8 >> 5).astype(F32), (from8 & 31).astype(F32)], index4, 8)
     cidx = (upper * 32.0 + lower).astype(I32)
-
+    turned = pltpu.roll(cidx, LANES // 2, 1)
+    cidx = jnp.where(iota(shape, 0) == 2, jnp.broadcast_to(turned[0:1, :], shape), cidx)
+
+    marks = number[3:4, :]
+    for r in range(4):
+        marks = jnp.where(iota((1, LANES), 1) == size["start_lane"] + r, -2.0 - starts[r], marks)
+    number = jnp.concatenate([number[0:3, :], marks], axis=0)
     number_ref[0:4, :] = number
     number_ref[4:8, :] = number
     i_put(state_i, "following", following)
@@ -408,21 +416,22 @@
     return result
 
 
-def expand_dense(size, load_row, number_rows, slots, dense):
+def expand_dense(size, load_row, slots, dense):
     X, Y, Z = size["mesh"]
     R = Y * Z
-    nq = len(slots)
+    lane = iota((R, LANES), 1)
     for x in range(X):
+        last = load_row("map", x, 3)
+        rows = {r: load_row("q", x, r) for r in sorted({r for slot in slots for r in slot[:2]})}
         for l in range(4):
-            number = load_row(number_rows, x, l)
-            high = number >> 7
+            number = load_row("map", x, l) if l < 3 else last
+            start = -2 - pick(last, jnp.full((R, LANES), size["start_lane"] + l, I32))
             low = number & 127
-            for i, q in enumerate(slots):
-                first, rest, half = q
-                a = pick(load_row("q", x, first), low)
-                b = pick(load_row("q", x, rest), (low & 63) + 64 * half)
-                value = jnp.where(number < 0, 0.0, jnp.where(high == 0, a, b))
-                dense[x, i, :, l * LANES:(l + 1) * LANES] = value
+            keep = [lane >= start, (lane < LANES // 2) | (lane - LANES // 2 >= start)]
+            for i, (first, rest, half) in enumerate(slots):
+                row = jnp.where(keep[half], rows[first], rows[rest])
+                value = pick(row, low ^ (half * (LANES // 2)))
+                dense[x, i, :, l * LANES:(l + 1) * LANES] = jnp.where(number < 0, 0.0, value)
 
 
 def aligned(size, dense, q, target, tile):
@@ -530,7 +539,7 @@
         row = plane(size, got2, x, size["map_row"] + r if kind == "map" else r, rows2)
         return row.astype(I32) if kind == "map" else row
 
-    expand_dense(size, load_row, "map", [(q, NQ + q // 2, q % 2) for q in range(NQ)], dense)
+    expand_dense(size, load_row, [(q, NQ + q // 2, q % 2) for q in range(NQ)], dense)
     scaled_tiles, total_tiles, own_total = [], [], None
     for t in range(3):
         target = lax.rem(gx + (t - 1 + X), X)
@@ -632,7 +641,7 @@
         return plane(size, [got3], x, r, 8)
 
     nk = ORDER + 1
-    expand_dense(size, load_row, "map", [(q, nk + q // 2, q % 2) for q in range(nk)], dense)
+    expand_dense(size, load_row, [(q, nk + q // 2, q % 2) for q in range(nk)], dense)
     scaled_tiles, own_total = [], None
     for t in range(3):
         target = lax.rem(gx + (t - 1 + X), X)
@@ -702,7 +711,7 @@
         bonds = bond_head.shape[-1]
         send = send_list.shape[-1]
         atom_rows = atoms // LANES
-        assert atoms % LANES == 0 and bonds == 8 * LANES and LANES % send == 0 and atom_rows <= 16
+        assert atoms % LANES == 0 and bonds == 8 * LANES and LANES % send == 0 and atom_rows <= 16 and 3 * LANES < 27 * send <= 4 * LANES - 4
         rows2 = NQ + (NQ + 1) // 2 + 4
 
         def load_send(ref):
@@ -710,7 +719,7 @@
             return jnp.concatenate([one] * (LANES // send), axis=1)
 
         size = dict(mesh=sizes, send=send, atom_rows=atom_rows, atom_pad=16, ext_rows=16, rows2=rows2,
-                    map_row=NQ + (NQ + 1) // 2, load_send=load_send,
+                    map_row=NQ + (NQ + 1) // 2, load_send=load_send, start_lane=27 * send - 3 * LANES,
                     atom_parts=[min(8, atom_rows), max(atom_rows - 8, 0)])
 
         def call(kernel, outs, scratch, *args, space=pltpu.VMEM):

time: 44.8 us -> 44.3 us (0.989)
  no operation moved by 1% of the time
where the time goes in v4:
time: 44.3 us; the launch traced here: 44.1 us
  blocking collectives  21.5 us (49%)
  waiting for transfers between devices  7.5 us (17%)
  starting transfers between devices  7.33 us (17%)
  Pallas kernels  7.06 us (16%)
  between operations  0.67 us (2%)
    all_to_all x2, blocking collectives, share(): lax.all_to_all(message, axes, split_axis=0, concat_axis=0, tiled=True)  21.5 us
    all_to_all x1, starting transfers between devices, share(): lax.all_to_all(message, axes, split_axis=0, concat_axis=0, tiled=True)  7.33 us
    pallas_call x5, Pallas kernels, call(): pl.pallas_call(wrapped, out_shape=outs, scratch_shapes=scratch, in_specs=...  7.06 us
    all_to_all x1, waiting for transfers between devices, share(): lax.all_to_all(message, axes, split_axis=0, concat_axis=0, tiled=True)  6.1 us
    ppermute x1, waiting for transfers between devices, per_device(): lax.ppermute(got2, 'gy', [((i + k) % Y, i) for i in range(Y)])  1.4 us
  transfers between devices with their start and end apart: 2, of which 2 were waited for; matrix products, arithmetic and copies ran while one was open for 0% of the time, Pallas kernels for 2%

profile of v4, /device:TPU:0, one launch (start us, length us, event | category | flops | bytes accessed | tf_op | source)
XLA Modules:
  0.0 44.1 jit_solution(3464914932308769756)
XLA Ops:
  0.6 1.6 %shard_map.77 = (f32[32,1,128]{2,1,0:T(1,128)}, f32[112,128]{1,0:T(8,128)S(1)}, s32[24,128]{1,0:T(8,128)S(1)}) custom-call(f32[3,1,1,1,1536]{4,3,2,1,0:T(1,128)} %refs_0_.1, f32[3,1,1,1,1536]{4,3,2,1,0:T(1,128)} %refs_1_.1, f32[1,1,1,1536]{3,2,1,0:T(1,128)} %refs_2_.1, s32[1,1,1,1024]{3,2,1,0:T(1,128)} %refs_3_.1, s32[1,1,1,1024]{3,2,1,0:T(1,128)} %refs_4_.1, ...), custom_call_target="tpu_custom_call" | custom-call | tf_op jit(solution)/shard_map/pallas_call | solution.py:729
  2.2 7.3 %all-to-all-start = ((f32[32,1,128]{2,1,0:T(1,128)}), f32[32,1,128]{2,1,0:T(1,128)S(1)}, u32[]{:S(2)}, u32[]{:S(2)}) async-start(f32[32,1,128]{2,1,0:T(1,128)} %get-tuple-element.22), calls=%async_computation | async-start | bytes 32768 | tf_op jit(solution)/shard_map/all_to_all | solution.py:700
  9.6 1.0 %shard_map.78 = (s32[96,128]{1,0:T(8,128)S(1)}, f32[8,128]{1,0:T(8,128)S(1)}, f32[56,128]{1,0:T(8,128)S(1)}, f32[56,128]{1,0:T(8,128)S(1)}) custom-call(f32[112,128]{1,0:T(8,128)S(1)} %get-tuple-element.16.refs_0_, s32[24,128]{1,0:T(8,128)S(1)} %get-tuple-element.17.refs_1_), custom_call_target="tpu_custom_call" | custom-call | tf_op jit(solution)/shard_map/pallas_call | solution.py:729
  10.6 6.1 %all-to-all-done.refs_4_ = f32[32,1,128]{2,1,0:T(1,128)S(1)} async-done(((f32[32,1,128]{2,1,0:T(1,128)}), f32[32,1,128]{2,1,0:T(1,128)S(1)}, u32[]{:S(2)}, u32[]{:S(2)}) %all-to-all-start) | async-done | bytes 16416 | tf_op jit(solution)/shard_map/all_to_all | solution.py:700
  16.7 1.0 %shard_map.79 = (f32[136,128]{1,0:T(8,128)S(1)}, f32[16,21,1,128]{3,2,1,0:T(1,128)S(1)}) custom-call(s32[96,128]{1,0:T(8,128)S(1)} %get-tuple-element.18.refs_0_.refs_1_.refs_2_, f32[8,128]{1,0:T(8,128)S(1)} %get-tuple-element.19.refs_1_, f32[56,128]{1,0:T(8,128)S(1)} %get-tuple-element.20.refs_2_, f32[56,128]{1,0:T(8,128)S(1)} %get-tuple-element.21.refs_3_, ...), custom_call_target="tpu_custom_call" | custom-call | tf_op jit(solution)/shard_map/pallas_call | solution.py:729
  17.7 11.4 %all_to_all.15 = f32[16,21,1,128]{3,2,1,0:T(1,128)S(1)} all-to-all(f32[16,21,1,128]{3,2,1,0:T(1,128)S(1)} %get-tuple-element.24), channel_id=1, replica_groups=mesh['gx'=4,'gy'=2,'gz'=4] {'gx','gz'}, dimensions={0} | all-to-all | bytes 344064 | tf_op jit(solution)/shard_map/all_to_all | solution.py:700
  29.1 0.0 collective-permute-start
  29.1 1.4 %collective-permute-done = f32[16,21,1,128]{3,2,1,0:T(1,128)S(1)} collective-permute-done((f32[16,21,1,128]{3,2,1,0:T(1,128)S(1)}, f32[16,21,1,128]{3,2,1,0:T(1,128)S(1)}, u32[]{:S(2)}, u32[]{:S(2)}) %collective-permute-start) | collective-permute-done | bytes 172064 | tf_op jit(solution)/shard_map/ppermute | solution.py:754
  30.6 1.8 %shard_map.80 = (f32[32,8,128]{2,1,0:T(8,128)S(1)}, f32[16,128]{1,0:T(8,128)S(1)}, f32[3,3,8,512]{3,2,1,0:T(8,128)S(1)}, f32[3,25,8,128]{3,2,1,0:T(8,128)S(1)}, f32[24,128]{1,0:T(8,128)S(1)}) custom-call(f32[136,128]{1,0:T(8,128)S(1)} %get-tuple-element.23.refs_0_.refs_1_, s32[96,128]{1,0:T(8,128)S(1)} %get-tuple-element.18.refs_0_.refs_1_.refs_2_, ...), custom_call_target="tpu_custom_call" | custom-call | tf_op jit(solution)/shard_map/pallas_call | solution.py:729
  32.4 10.1 %all_to_all.16 = f32[32,8,128]{2,1,0:T(8,128)S(1)} all-to-all(f32[32,8,128]{2,1,0:T(8,128)S(1)} %get-tuple-element.25), channel_id=1, replica_groups=mesh['gx'=4,'gy'=2,'gz'=4] {'gx','gy','gz'}, dimensions={0} | all-to-all | bytes 262144 | tf_op jit(solution)/shard_map/all_to_all | solution.py:700
  42.5 1.6 %shard_map.81 = (f32[3,1,1,1,1536]{4,3,2,1,0:T(1,128)}, f32[1,1,1,1024]{3,2,1,0:T(1,128)}) custom-call(f32[112,128]{1,0:T(8,128)S(1)} %get-tuple-element.16.refs_0_, f32[136,128]{1,0:T(8,128)S(1)} %get-tuple-element.23.refs_0_.refs_1_, s32[96,128]{1,0:T(8,128)S(1)} %get-tuple-element.18.refs_0_.refs_1_.refs_2_, f32[256,128]{1,0:T(8,128)S(1)} %bitcast.8, ...), custom_call_target="tpu_custom_call" | custom-call | tf_op jit(solution)/shard_map/pallas_call | solution.py:729
Async XLA Ops:
  2.2 14.5 %all-to-all-start = ((f32[32,1,128]{2,1,0:T(1,128)}), f32[32,1,128]{2,1,0:T(1,128)S(1)}, u32[]{:S(2)}, u32[]{:S(2)}) async-start(f32[32,1,128]{2,1,0:T(1,128)} %get-tuple-element.22), calls=%async_computation | async-start | bytes 32768 | tf_op jit(solution)/shard_map/all_to_all | solution.py:700
  29.1 1.4 %collective-permute-start = (f32[16,21,1,128]{3,2,1,0:T(1,128)S(1)}, f32[16,21,1,128]{3,2,1,0:T(1,128)S(1)}, u32[]{:S(2)}, u32[]{:S(2)}) collective-permute-start(f32[16,21,1,128]{3,2,1,0:T(1,128)S(1)} %all_to_all.15), channel_id=1, source_target_pairs={{4,0},{0,4},{5,1},{1,5},{6,2},{2,6},{7,3},{3,7},{12,8},{8,12},{13,... | collective-permute-start | bytes 516104 | tf_op jit(solution)/shard_map/ppermute | solution.py:754

commit v5 on v4

--- a/solution.py
+++ b/solution.py
@@ -24,6 +24,10 @@
 
 def pick(table, index):
     return jnp.take_along_axis(table, index, axis=1, mode="promise_in_bounds")
+
+
+def pick_row(table, index):
+    return jnp.take_along_axis(table, index, axis=0, mode="promise_in_bounds")
 
 
 def spread_row(row, like):
@@ -389,13 +393,18 @@
             f_put(state_f, f"g{k}", summed)
         rows = compact_rows(force + unit[1:] + terms, cidx)
         rows = rows + value_rows(number_ref[0:4, :])
-        for r, row in enumerate(rows):
-            out_ref[0, r, :, :] = row
+        part_rows = size["part_rows"]
+        rows = rows + [rows[-1]] * (Y * part_rows - len(rows))
+        for k in range(Y):
+            row_y = lax.rem(lax.axis_index("gy") + k, Y)
+            for r in range(0, part_rows, 8):
+                some = rows[k * part_rows + r:k * part_rows + min(r + 8, part_rows)]
+                block = jnp.concatenate(some, axis=0)
+                for x in range(X):
+                    for z in range(Z):
+                        out_ref[(x * Y + row_y) * Z + z, r:r + len(some), 0, :] = block
 
     both_ways(extra, run)
-    for d in range(1, out_ref.shape[0]):
-        for r in range(size["rows2"]):
-            out_ref[d, r, :, :] = out_ref[0, r, :, :]
 
 
 def lane_fields(tile):
@@ -444,6 +453,10 @@
     offs = [sorted({OFFSETS[b][k] for b in blocks}) for k in range(3)]
     value = choose({o: dense[lax.rem(target + (X - o), X), q, :, span] for o in offs[0]}, dx, offs[0])
     row_z = iota((R, LANES), 0) % Z
+    if R == 8:
+        row_y = iota((R, LANES), 0) // Z
+        source = lax.rem(row_y - dy + Y, Y) * Z + lax.rem(row_z - dz + Z, Z)
+        return pick_row(value, source)
     options = {0: value}
     if 1 in offs[2]:
         options[1] = jnp.where(row_z == 0, turn(value, Z - 1, R), turn(value, -1, R))
@@ -462,11 +475,11 @@
 def lane_totals(sums, send):
     stack = jnp.concatenate([parts[0] + parts[1] + parts[2] + parts[3] for parts in sums.values()], axis=0)
     pieces = []
-    for _ in range(3):
+    for _ in range(2):
         piece = stack.astype(jnp.bfloat16)
         pieces.append(piece)
         stack = stack - piece.astype(F32)
-    same = iota((3 * LANES, LANES), 0) % send == iota((3 * LANES, LANES), 1) % send
+    same = iota((2 * LANES, LANES), 0) % send == iota((2 * LANES, LANES), 1) % send
     table = jnp.dot(jnp.concatenate(pieces, axis=1), jnp.where(same, 1.0, 0.0).astype(jnp.bfloat16),
                     preferred_element_type=F32)
     rows = table.shape[0] // len(sums)
@@ -504,6 +517,8 @@
     wanted = lax.rem(dy + Y, Y) * Z + lax.rem(gz + dz + Z, Z)
     offs = sorted({OFFSETS[b][0] for b in blocks})
     value = choose({o: tiles[o + 1] for o in offs}, dx, offs)
+    if R == 8:
+        return pick_row(value, wanted)[0:1]
     return jnp.sum(jnp.where(wanted == iota((R, LANES), 0), value, 0.0), axis=0, keepdims=True)
 
 
@@ -519,10 +534,13 @@
     gy = lax.axis_index("gy")
     pieces = []
     for k in range(Y):
-        if len(refs) > 1:
-            pieces.append(strided(refs[k], x * Z * stride + row, Z, stride))
+        first = (x * Y + lax.rem(gy + k, Y)) * Z
+        if stride is None:
+            part_rows = size["part_rows"]
+            ref = refs[(row // part_rows + k) % Y]
+            pieces.append(strided(ref, first * part_rows + row % part_rows, Z, part_rows))
         else:
-            pieces.append(strided(refs[0], (x * Y + lax.rem(gy + k, Y)) * Z * stride + row, Z, stride))
+            pieces.append(strided(refs[0], first * stride + row, Z, stride))
     return jnp.concatenate(pieces, axis=0)
 
 
@@ -531,12 +549,11 @@
     X, Y, Z = size["mesh"]
     send = size["send"]
     R = Y * Z
-    rows2 = size["rows2"]
     place = my_place()
     gx, gy, gz = place
 
     def load_row(kind, x, r):
-        row = plane(size, got2, x, size["map_row"] + r if kind == "map" else r, rows2)
+        row = plane(size, got2, x, size["map_row"] + r if kind == "map" else r, None)
         return row.astype(I32) if kind == "map" else row
 
     expand_dense(size, load_row, [(q, NQ + q // 2, q % 2) for q in range(NQ)], dense)
@@ -631,13 +648,12 @@
     X, Y, Z = size["mesh"]
     send = size["send"]
     R = Y * Z
-    rows2 = size["rows2"]
     place = my_place()
     gx, gy, gz = place
 
     def load_row(kind, x, r):
         if kind == "map":
-            return plane(size, got2, x, size["map_row"] + r, rows2).astype(I32)
+            return plane(size, got2, x, size["map_row"] + r, None).astype(I32)
         return plane(size, [got3], x, r, 8)
 
     nk = ORDER + 1
@@ -696,8 +712,8 @@
     both_ways(extra, run)
 
 
-def share(message, axes=AXES):
-    return lax.all_to_all(message, axes, split_axis=0, concat_axis=0, tiled=True)
+def share(message):
+    return lax.all_to_all(message, AXES, split_axis=0, concat_axis=0, tiled=True)
 
 
 def make_per_device(mesh):
@@ -713,12 +729,13 @@
         atom_rows = atoms // LANES
         assert atoms % LANES == 0 and bonds == 8 * LANES and LANES % send == 0 and atom_rows <= 16 and 3 * LANES < 27 * send <= 4 * LANES - 4
         rows2 = NQ + (NQ + 1) // 2 + 4
+        part_rows = -(-rows2 // Y)
 
         def load_send(ref):
             one = ref[0, 0, 0:1, :]
             return jnp.concatenate([one] * (LANES // send), axis=1)
 
-        size = dict(mesh=sizes, send=send, atom_rows=atom_rows, atom_pad=16, ext_rows=16, rows2=rows2,
+        size = dict(mesh=sizes, send=send, atom_rows=atom_rows, atom_pad=16, ext_rows=16, part_rows=part_rows,
                     map_row=NQ + (NQ + 1) // 2, load_send=load_send, start_lane=27 * send - 3 * LANES,
                     atom_parts=[min(8, atom_rows), max(atom_rows - 8, 0)])
 
@@ -747,12 +764,12 @@
             [pltpu.VMEM((16, LANES), I32)], table, cons)
         state_f, two = call(
             geometry_kernel,
-            (S((8 * len(F_NAMES), LANES), F32), S((X * Z, rows2, 1, LANES), F32)),
+            (S((8 * len(F_NAMES), LANES), F32), S((devices, part_rows, 1, LANES), F32)),
             [pltpu.VMEM((32, LANES), F32), pltpu.VMEM((32, LANES), F32)],
             state_i, number, head_at, tail_at, got1)
-        got2 = share(two, ("gx", "gz"))
+        got2 = share(two)
         got2 = [got2] + [lax.ppermute(got2, "gy", [((i + k) % Y, i) for i in range(Y)]) for k in range(1, Y)]
-        got2 = [g.reshape(X * Z * rows2, LANES) for g in got2]
+        got2 = [g.reshape(devices * part_rows, LANES) for g in got2]
         wide = 4 * LANES
         three, pair, force, matrix, keep = call(
             middle_kernel,

time: 44.3 us -> 43.6 us (0.984)
  blocking collectives: 21.5 us -> 21 us
    all_to_all x2, blocking collectives: 21.5 us -> 21 us  [share(): lax.all_to_all(message, AXES, split_axis=0, concat_axis=0, tiled=True)]
where the time goes in v5:
time: 43.6 us; the launch traced here: 43.3 us
  blocking collectives  21 us (48%)
  waiting for transfers between devices  7.52 us (17%)
  starting transfers between devices  7.33 us (17%)
  Pallas kernels  6.78 us (16%)
  between operations  0.67 us (2%)
    all_to_all x2, blocking collectives, share(): lax.all_to_all(message, AXES, split_axis=0, concat_axis=0, tiled=True)  21 us
    all_to_all x1, starting transfers between devices, share(): lax.all_to_all(message, AXES, split_axis=0, concat_axis=0, tiled=True)  7.33 us
    pallas_call x5, Pallas kernels, call(): pl.pallas_call(wrapped, out_shape=outs, scratch_shapes=scratch, in_specs=...  6.78 us
    all_to_all x1, waiting for transfers between devices, share(): lax.all_to_all(message, AXES, split_axis=0, concat_axis=0, tiled=True)  6.1 us
    ppermute x1, waiting for transfers between devices, per_device(): lax.ppermute(got2, 'gy', [((i + k) % Y, i) for i in range(Y)])  1.42 us
  transfers between devices with their start and end apart: 2, of which 2 were waited for; matrix products, arithmetic and copies ran while one was open for 0% of the time, Pallas kernels for 2%

profile of v5, /device:TPU:0, one launch (start us, length us, event | category | flops | bytes accessed | tf_op | source)
XLA Modules:
  0.0 43.3 jit_solution(12058451822510726818)
XLA Ops:
  0.6 1.6 %shard_map.77 = (f32[32,1,128]{2,1,0:T(1,128)}, f32[112,128]{1,0:T(8,128)S(1)}, s32[24,128]{1,0:T(8,128)S(1)}) custom-call(f32[3,1,1,1,1536]{4,3,2,1,0:T(1,128)} %refs_0_.1, f32[3,1,1,1,1536]{4,3,2,1,0:T(1,128)} %refs_1_.1, f32[1,1,1,1536]{3,2,1,0:T(1,128)} %refs_2_.1, s32[1,1,1,1024]{3,2,1,0:T(1,128)} %refs_3_.1, s32[1,1,1,1024]{3,2,1,0:T(1,128)} %refs_4_.1, ...), custom_call_target="tpu_custom_call" | custom-call | tf_op jit(solution)/shard_map/pallas_call | solution.py:746
  2.2 7.3 %all-to-all-start = ((f32[32,1,128]{2,1,0:T(1,128)}), f32[32,1,128]{2,1,0:T(1,128)S(1)}, u32[]{:S(2)}, u32[]{:S(2)}) async-start(f32[32,1,128]{2,1,0:T(1,128)} %get-tuple-element.22), calls=%async_computation | async-start | bytes 32768 | tf_op jit(solution)/shard_map/all_to_all | solution.py:716
  9.6 1.0 %shard_map.78 = (s32[96,128]{1,0:T(8,128)S(1)}, f32[8,128]{1,0:T(8,128)S(1)}, f32[56,128]{1,0:T(8,128)S(1)}, f32[56,128]{1,0:T(8,128)S(1)}) custom-call(f32[112,128]{1,0:T(8,128)S(1)} %get-tuple-element.16.refs_0_, s32[24,128]{1,0:T(8,128)S(1)} %get-tuple-element.17.refs_1_), custom_call_target="tpu_custom_call" | custom-call | tf_op jit(solution)/shard_map/pallas_call | solution.py:746
  10.6 6.1 %all-to-all-done.refs_4_ = f32[32,1,128]{2,1,0:T(1,128)S(1)} async-done(((f32[32,1,128]{2,1,0:T(1,128)}), f32[32,1,128]{2,1,0:T(1,128)S(1)}, u32[]{:S(2)}, u32[]{:S(2)}) %all-to-all-start) | async-done | bytes 16416 | tf_op jit(solution)/shard_map/all_to_all | solution.py:716
  16.7 1.0 %shard_map.79 = (f32[136,128]{1,0:T(8,128)S(1)}, f32[32,11,1,128]{3,2,1,0:T(1,128)S(1)}) custom-call(s32[96,128]{1,0:T(8,128)S(1)} %get-tuple-element.18.refs_0_.refs_1_.refs_2_, f32[8,128]{1,0:T(8,128)S(1)} %get-tuple-element.19.refs_1_, f32[56,128]{1,0:T(8,128)S(1)} %get-tuple-element.20.refs_2_, f32[56,128]{1,0:T(8,128)S(1)} %get-tuple-element.21.refs_3_, ...), custom_call_target="tpu_custom_call" | custom-call | tf_op jit(solution)/shard_map/pallas_call | solution.py:746
  17.7 10.8 %all_to_all.15 = f32[32,11,1,128]{3,2,1,0:T(1,128)S(1)} all-to-all(f32[32,11,1,128]{3,2,1,0:T(1,128)S(1)} %get-tuple-element.24), channel_id=1, replica_groups=mesh['gx'=4,'gy'=2,'gz'=4] {'gx','gy','gz'}, dimensions={0} | all-to-all | bytes 360448 | tf_op jit(solution)/shard_map/all_to_all | solution.py:716
  28.5 0.0 collective-permute-start
  28.5 1.4 %collective-permute-done = f32[32,11,1,128]{3,2,1,0:T(1,128)S(1)} collective-permute-done((f32[32,11,1,128]{3,2,1,0:T(1,128)S(1)}, f32[32,11,1,128]{3,2,1,0:T(1,128)S(1)}, u32[]{:S(2)}, u32[]{:S(2)}) %collective-permute-start) | collective-permute-done | bytes 180256 | tf_op jit(solution)/shard_map/ppermute | solution.py:771
  29.9 1.6 %shard_map.80 = (f32[32,8,128]{2,1,0:T(8,128)S(1)}, f32[16,128]{1,0:T(8,128)S(1)}, f32[3,3,8,512]{3,2,1,0:T(8,128)S(1)}, f32[3,25,8,128]{3,2,1,0:T(8,128)S(1)}, f32[24,128]{1,0:T(8,128)S(1)}) custom-call(f32[136,128]{1,0:T(8,128)S(1)} %get-tuple-element.23.refs_0_.refs_1_, s32[96,128]{1,0:T(8,128)S(1)} %get-tuple-element.18.refs_0_.refs_1_.refs_2_, ...), custom_call_target="tpu_custom_call" | custom-call | tf_op jit(solution)/shard_map/pallas_call | solution.py:746
  31.5 10.2 %all_to_all.16 = f32[32,8,128]{2,1,0:T(8,128)S(1)} all-to-all(f32[32,8,128]{2,1,0:T(8,128)S(1)} %get-tuple-element.25), channel_id=1, replica_groups=mesh['gx'=4,'gy'=2,'gz'=4] {'gx','gy','gz'}, dimensions={0} | all-to-all | bytes 262144 | tf_op jit(solution)/shard_map/all_to_all | solution.py:716
  41.8 1.6 %shard_map.81 = (f32[3,1,1,1,1536]{4,3,2,1,0:T(1,128)}, f32[1,1,1,1024]{3,2,1,0:T(1,128)}) custom-call(f32[112,128]{1,0:T(8,128)S(1)} %get-tuple-element.16.refs_0_, f32[136,128]{1,0:T(8,128)S(1)} %get-tuple-element.23.refs_0_.refs_1_, s32[96,128]{1,0:T(8,128)S(1)} %get-tuple-element.18.refs_0_.refs_1_.refs_2_, f32[256,128]{1,0:T(8,128)S(1)} %bitcast.8, ...), custom_call_target="tpu_custom_call" | custom-call | tf_op jit(solution)/shard_map/pallas_call | solution.py:746
Async XLA Ops:
  2.2 14.5 %all-to-all-start = ((f32[32,1,128]{2,1,0:T(1,128)}), f32[32,1,128]{2,1,0:T(1,128)S(1)}, u32[]{:S(2)}, u32[]{:S(2)}) async-start(f32[32,1,128]{2,1,0:T(1,128)} %get-tuple-element.22), calls=%async_computation | async-start | bytes 32768 | tf_op jit(solution)/shard_map/all_to_all | solution.py:716
  28.5 1.4 %collective-permute-start = (f32[32,11,1,128]{3,2,1,0:T(1,128)S(1)}, f32[32,11,1,128]{3,2,1,0:T(1,128)S(1)}, u32[]{:S(2)}, u32[]{:S(2)}) collective-permute-start(f32[32,11,1,128]{3,2,1,0:T(1,128)S(1)} %all_to_all.15), channel_id=1, source_target_pairs={{4,0},{0,4},{5,1},{1,5},{6,2},{2,6},{7,3},{3,7},{12,8},{8,12},{13,... | collective-permute-start | bytes 540680 | tf_op jit(solution)/shard_map/ppermute | solution.py:771

commit v6 on v5

--- a/solution.py
+++ b/solution.py
@@ -303,6 +303,7 @@
     marks = number[3:4, :]
     for r in range(4):
         marks = jnp.where(iota((1, LANES), 1) == size["start_lane"] + r, -2.0 - starts[r], marks)
+    marks = pltpu.roll(jnp.broadcast_to(marks, shape), LANES // 2, 1)[0:1, :]
     number = jnp.concatenate([number[0:3, :], marks], axis=0)
     number_ref[0:4, :] = number
     number_ref[4:8, :] = number
@@ -392,7 +393,8 @@
             summed = summed + unit[k]
             f_put(state_f, f"g{k}", summed)
         rows = compact_rows(force + unit[1:] + terms, cidx)
-        rows = rows + value_rows(number_ref[0:4, :])
+        rows[-1] = jnp.where(iota((1, LANES), 1) < LANES // 2, rows[-1], number_ref[3:4, :])
+        rows = rows + value_rows(number_ref[0:3, :])
         part_rows = size["part_rows"]
         rows = rows + [rows[-1]] * (Y * part_rows - len(rows))
         for k in range(Y):
@@ -431,10 +433,11 @@
     lane = iota((R, LANES), 1)
     for x in range(X):
         last = load_row("map", x, 3)
+        marks = load_row("mark", x, 0)
         rows = {r: load_row("q", x, r) for r in sorted({r for slot in slots for r in slot[:2]})}
         for l in range(4):
             number = load_row("map", x, l) if l < 3 else last
-            start = -2 - pick(last, jnp.full((R, LANES), size["start_lane"] + l, I32))
+            start = -2 - pick(marks, jnp.full((R, LANES), LANES // 2 + size["start_lane"] + l, I32)).astype(I32)
             low = number & 127
             keep = [lane >= start, (lane < LANES // 2) | (lane - LANES // 2 >= start)]
             for i, (first, rest, half) in enumerate(slots):
@@ -544,6 +547,14 @@
     return jnp.concatenate(pieces, axis=0)
 
 
+def map_row(size, refs, x, tile):
+    if tile < 3:
+        return plane(size, refs, x, size["map_row"] + tile, None).astype(I32)
+    row = plane(size, refs, x, size["map_row"] - 1, None)
+    lane = iota(row.shape, 1)
+    return jnp.where(lane < LANES // 2, pick(row, lane ^ (LANES // 2)), -1.0).astype(I32)
+
+
 def middle_kernel(size, state_f, state_i, got1, *refs):
     *got2, out_ref, pair_ref, force_ref, matrix_ref, keep_ref, dense = refs
     X, Y, Z = size["mesh"]
@@ -553,8 +564,9 @@
     gx, gy, gz = place
 
     def load_row(kind, x, r):
-        row = plane(size, got2, x, size["map_row"] + r if kind == "map" else r, None)
-        return row.astype(I32) if kind == "map" else row
+        if kind == "mark":
+            return plane(size, got2, x, size["map_row"] - 1, None)
+        return map_row(size, got2, x, r) if kind == "map" else plane(size, got2, x, r, None)
 
     expand_dense(size, load_row, [(q, NQ + q // 2, q % 2) for q in range(NQ)], dense)
     scaled_tiles, total_tiles, own_total = [], [], None
@@ -652,9 +664,9 @@
     gx, gy, gz = place
 
     def load_row(kind, x, r):
-        if kind == "map":
-            return plane(size, got2, x, size["map_row"] + r, None).astype(I32)
-        return plane(size, [got3], x, r, 8)
+        if kind == "mark":
+            return plane(size, got2, x, size["map_row"] - 1, None)
+        return map_row(size, got2, x, r) if kind == "map" else plane(size, [got3], x, r, 8)
 
     nk = ORDER + 1
     expand_dense(size, load_row, [(q, nk + q // 2, q % 2) for q in range(nk)], dense)
@@ -727,8 +739,9 @@
         bonds = bond_head.shape[-1]
         send = send_list.shape[-1]
         atom_rows = atoms // LANES
-        assert atoms % LANES == 0 and bonds == 8 * LANES and LANES % send == 0 and atom_rows <= 16 and 3 * LANES < 27 * send <= 4 * LANES - 4
-        rows2 = NQ + (NQ + 1) // 2 + 4
+        assert atoms % LANES == 0 and bonds == 8 * LANES and LANES % send == 0 and atom_rows <= 16 and 3 * LANES < 27 * send <= 3 * LANES + LANES // 2 - 4
+        rows2 = NQ + (NQ + 1) // 2 + 3
+        assert NQ % 2 == 1
         part_rows = -(-rows2 // Y)
 
         def load_send(ref):

time: 43.6 us -> 43.2 us (level)
  no operation moved by 1% of the time
where the time goes in v6:
time: 43.2 us; the launch traced here: 42.9 us
  blocking collectives  20.7 us (48%)
  waiting for transfers between devices  7.58 us (18%)
  starting transfers between devices  7.33 us (17%)
  Pallas kernels  6.69 us (15%)
  between operations  0.66 us (2%)
    all_to_all x2, blocking collectives, share(): lax.all_to_all(message, AXES, split_axis=0, concat_axis=0, tiled=True)  20.7 us
    all_to_all x1, starting transfers between devices, share(): lax.all_to_all(message, AXES, split_axis=0, concat_axis=0, tiled=True)  7.33 us
    pallas_call x5, Pallas kernels, call(): pl.pallas_call(wrapped, out_shape=outs, scratch_shapes=scratch, in_specs=...  6.69 us
    all_to_all x1, waiting for transfers between devices, share(): lax.all_to_all(message, AXES, split_axis=0, concat_axis=0, tiled=True)  6.18 us
    ppermute x1, waiting for transfers between devices, per_device(): lax.ppermute(got2, 'gy', [((i + k) % Y, i) for i in range(Y)])  1.39 us
  transfers between devices with their start and end apart: 2, of which 2 were waited for; matrix products, arithmetic and copies ran while one was open for 0% of the time, Pallas kernels for 2%

profile of v6, /device:TPU:0, one launch (start us, length us, event | category | flops | bytes accessed | tf_op | source)
XLA Modules:
  0.0 42.9 jit_solution(12294183252027973217)
XLA Ops:
  0.6 1.6 %shard_map.77 = (f32[32,1,128]{2,1,0:T(1,128)}, f32[112,128]{1,0:T(8,128)S(1)}, s32[24,128]{1,0:T(8,128)S(1)}) custom-call(f32[3,1,1,1,1536]{4,3,2,1,0:T(1,128)} %refs_0_.1, f32[3,1,1,1,1536]{4,3,2,1,0:T(1,128)} %refs_1_.1, f32[1,1,1,1536]{3,2,1,0:T(1,128)} %refs_2_.1, s32[1,1,1,1024]{3,2,1,0:T(1,128)} %refs_3_.1, s32[1,1,1,1024]{3,2,1,0:T(1,128)} %refs_4_.1, ...), custom_call_target="tpu_custom_call" | custom-call | tf_op jit(solution)/shard_map/pallas_call | solution.py:759
  2.2 7.3 %all-to-all-start = ((f32[32,1,128]{2,1,0:T(1,128)}), f32[32,1,128]{2,1,0:T(1,128)S(1)}, u32[]{:S(2)}, u32[]{:S(2)}) async-start(f32[32,1,128]{2,1,0:T(1,128)} %get-tuple-element.22), calls=%async_computation | async-start | bytes 32768 | tf_op jit(solution)/shard_map/all_to_all | solution.py:728
  9.6 0.9 %shard_map.78 = (s32[96,128]{1,0:T(8,128)S(1)}, f32[8,128]{1,0:T(8,128)S(1)}, f32[56,128]{1,0:T(8,128)S(1)}, f32[56,128]{1,0:T(8,128)S(1)}) custom-call(f32[112,128]{1,0:T(8,128)S(1)} %get-tuple-element.16.refs_0_, s32[24,128]{1,0:T(8,128)S(1)} %get-tuple-element.17.refs_1_), custom_call_target="tpu_custom_call" | custom-call | tf_op jit(solution)/shard_map/pallas_call | solution.py:759
  10.5 6.2 %all-to-all-done.refs_4_ = f32[32,1,128]{2,1,0:T(1,128)S(1)} async-done(((f32[32,1,128]{2,1,0:T(1,128)}), f32[32,1,128]{2,1,0:T(1,128)S(1)}, u32[]{:S(2)}, u32[]{:S(2)}) %all-to-all-start) | async-done | bytes 16416 | tf_op jit(solution)/shard_map/all_to_all | solution.py:728
  16.7 1.0 %shard_map.79 = (f32[136,128]{1,0:T(8,128)S(1)}, f32[32,10,1,128]{3,2,1,0:T(1,128)S(1)}) custom-call(s32[96,128]{1,0:T(8,128)S(1)} %get-tuple-element.18.refs_0_.refs_1_.refs_2_, f32[8,128]{1,0:T(8,128)S(1)} %get-tuple-element.19.refs_1_, f32[56,128]{1,0:T(8,128)S(1)} %get-tuple-element.20.refs_2_, f32[56,128]{1,0:T(8,128)S(1)} %get-tuple-element.21.refs_3_, ...), custom_call_target="tpu_custom_call" | custom-call | tf_op jit(solution)/shard_map/pallas_call | solution.py:759
  17.7 10.6 %all_to_all.15 = f32[32,10,1,128]{3,2,1,0:T(1,128)S(1)} all-to-all(f32[32,10,1,128]{3,2,1,0:T(1,128)S(1)} %get-tuple-element.24), channel_id=1, replica_groups=mesh['gx'=4,'gy'=2,'gz'=4] {'gx','gy','gz'}, dimensions={0} | all-to-all | bytes 327680 | tf_op jit(solution)/shard_map/all_to_all | solution.py:728
  28.2 0.0 collective-permute-start
  28.2 1.4 %collective-permute-done = f32[32,10,1,128]{3,2,1,0:T(1,128)S(1)} collective-permute-done((f32[32,10,1,128]{3,2,1,0:T(1,128)S(1)}, f32[32,10,1,128]{3,2,1,0:T(1,128)S(1)}, u32[]{:S(2)}, u32[]{:S(2)}) %collective-permute-start) | collective-permute-done | bytes 163872 | tf_op jit(solution)/shard_map/ppermute | solution.py:784
  29.6 1.6 %shard_map.80 = (f32[32,8,128]{2,1,0:T(8,128)S(1)}, f32[16,128]{1,0:T(8,128)S(1)}, f32[3,3,8,512]{3,2,1,0:T(8,128)S(1)}, f32[3,25,8,128]{3,2,1,0:T(8,128)S(1)}, f32[24,128]{1,0:T(8,128)S(1)}) custom-call(f32[136,128]{1,0:T(8,128)S(1)} %get-tuple-element.23.refs_0_.refs_1_, s32[96,128]{1,0:T(8,128)S(1)} %get-tuple-element.18.refs_0_.refs_1_.refs_2_, ...), custom_call_target="tpu_custom_call" | custom-call | tf_op jit(solution)/shard_map/pallas_call | solution.py:759
  31.3 10.1 %all_to_all.16 = f32[32,8,128]{2,1,0:T(8,128)S(1)} all-to-all(f32[32,8,128]{2,1,0:T(8,128)S(1)} %get-tuple-element.25), channel_id=1, replica_groups=mesh['gx'=4,'gy'=2,'gz'=4] {'gx','gy','gz'}, dimensions={0} | all-to-all | bytes 262144 | tf_op jit(solution)/shard_map/all_to_all | solution.py:728
  41.4 1.5 %shard_map.81 = (f32[3,1,1,1,1536]{4,3,2,1,0:T(1,128)}, f32[1,1,1,1024]{3,2,1,0:T(1,128)}) custom-call(f32[112,128]{1,0:T(8,128)S(1)} %get-tuple-element.16.refs_0_, f32[136,128]{1,0:T(8,128)S(1)} %get-tuple-element.23.refs_0_.refs_1_, s32[96,128]{1,0:T(8,128)S(1)} %get-tuple-element.18.refs_0_.refs_1_.refs_2_, f32[256,128]{1,0:T(8,128)S(1)} %bitcast.8, ...), custom_call_target="tpu_custom_call" | custom-call | tf_op jit(solution)/shard_map/pallas_call | solution.py:759
Async XLA Ops:
  2.2 14.5 %all-to-all-start = ((f32[32,1,128]{2,1,0:T(1,128)}), f32[32,1,128]{2,1,0:T(1,128)S(1)}, u32[]{:S(2)}, u32[]{:S(2)}) async-start(f32[32,1,128]{2,1,0:T(1,128)} %get-tuple-element.22), calls=%async_computation | async-start | bytes 32768 | tf_op jit(solution)/shard_map/all_to_all | solution.py:728
  28.2 1.4 %collective-permute-start = (f32[32,10,1,128]{3,2,1,0:T(1,128)S(1)}, f32[32,10,1,128]{3,2,1,0:T(1,128)S(1)}, u32[]{:S(2)}, u32[]{:S(2)}) collective-permute-start(f32[32,10,1,128]{3,2,1,0:T(1,128)S(1)} %all_to_all.15), channel_id=1, source_target_pairs={{4,0},{0,4},{5,1},{1,5},{6,2},{2,6},{7,3},{3,7},{12,8},{8,12},{13,... | collective-permute-start | bytes 491528 | tf_op jit(solution)/shard_map/ppermute | solution.py:784

commit v7 on v6

--- a/solution.py
+++ b/solution.py
@@ -142,12 +142,15 @@
         self.e, self.diag, self.kappa, self.tail_mass = direction, diag, kappa, tail_mass
         self.following, self.child, self.prev, self.last = following, child, prev, last
         self.extra, self.many = extra, many
+        self.child_kappa = None if many else gather_value(kappa, child)
 
     def total(self, value):
         return chain_sum(value, self.prev, self.extra) if self.many else value
 
     def apply(self, value):
         result = self.diag * value + self.kappa * gather_value(value, self.following)
+        if not self.many:
+            return result + self.child_kappa * gather_value(value, self.child)
         result = result + gather_value(self.total(self.kappa * value), self.child)
         if self.many:
             for d in range(3):
@@ -155,6 +158,32 @@
                 others = gather_value(self.total(force), self.last) - force
                 result = result - jnp.where(self.last >= 0, self.tail_mass * self.e[d] * others, 0.0)
         return result
+
+    def powers(self, value):
+        terms = [value]
+        if self.many or ORDER != 4:
+            for _ in range(ORDER):
+                terms.append(self.apply(terms[-1]))
+            return terms
+        n, c, k, d, kc = self.following, self.child, self.kappa, self.diag, self.child_kappa
+        n2 = gather_value(n + 1, n) - 1
+        c2 = gather_value(c + 1, c) - 1
+        far_n = k * gather_value(k, n)
+        far_c = kc * gather_value(kc, c)
+        near_n = k * (d + gather_value(d, n))
+        near_c = kc * (d + gather_value(d, c))
+        own = d * d + k * k + kc * kc
+
+        def twice(u, u_n, u_c):
+            return (own * u + near_n * u_n + near_c * u_c) + (
+                far_n * gather_value(u, n2) + far_c * gather_value(u, c2))
+
+        u_n, u_c = gather_value(value, n), gather_value(value, c)
+        one = d * value + k * u_n + kc * u_c
+        two = twice(value, u_n, u_c)
+        three = twice(one, gather_value(one, n), gather_value(one, c))
+        four = twice(two, gather_value(two, n), gather_value(two, c))
+        return [value, one, two, three, four]
 
     def at_head(self, force):
         return force - gather_value(self.total(force), self.child)
@@ -339,13 +368,11 @@
     for b, (dx, dy, dz) in enumerate(OFFSETS):
         at = (lax.rem(gx + (dx + X), X) * Y + lax.rem(gy + (dy + Y), Y)) * Z + lax.rem(gz + (dz + Z), Z)
         remote[b:b + 1, :] = got_ref[at, :, :]
-    sub, lane = iota(shape, 0), iota(shape, 1)
-    own = lane // send == sub
+    lane = iota(shape, 1)
     for j in range(4):
         block = remote[8 * j:8 * j + 8, :]
         for q in range(7):
-            got = jnp.where(own, pick(block, q * send + lane % send), 0.0)
-            row = jnp.sum(got, axis=0, keepdims=True)
+            row = pick_row(pick(block, q * send + lane % send), lane // send % 8)[0:1]
             rtab[4 * q + j:4 * q + j + 1, :] = row
     slot_high, slot_low = slot >> 7, slot & 127
     head_at = [head_ref[8 * q:8 * q + 8, :] for q in range(7)]
@@ -638,9 +665,7 @@
         length = f_get(state_f, "length")
         current = stretch[0] * stretch[0] + stretch[1] * stretch[1] + stretch[2] * stretch[2]
         target = jnp.sqrt(jnp.maximum(2.0 * length * length - current, 0.5 * length * length))
-        terms = [f_get(state_f, "scale") * (length - target)]
-        for _ in range(ORDER):
-            terms.append(operator.apply(terms[-1]))
+        terms = operator.powers(f_get(state_f, "scale") * (length - target))
         base = terms[0]
         for term in terms[1:]:
             base = base + term

time: 43.2 us -> 43.1 us (level)
  no operation moved by 1% of the time
where the time goes in v7:
time: 43.1 us; the launch traced here: 42.8 us
  blocking collectives  20.7 us (48%)
  waiting for transfers between devices  7.58 us (18%)
  starting transfers between devices  7.33 us (17%)
  Pallas kernels  6.59 us (15%)
  between operations  0.67 us (2%)
    all_to_all x2, blocking collectives, share(): lax.all_to_all(message, AXES, split_axis=0, concat_axis=0, tiled=True)  20.7 us
    all_to_all x1, starting transfers between devices, share(): lax.all_to_all(message, AXES, split_axis=0, concat_axis=0, tiled=True)  7.33 us
    pallas_call x5, Pallas kernels, call(): pl.pallas_call(wrapped, out_shape=outs, scratch_shapes=scratch, in_specs=...  6.59 us
    all_to_all x1, waiting for transfers between devices, share(): lax.all_to_all(message, AXES, split_axis=0, concat_axis=0, tiled=True)  6.18 us
    ppermute x1, waiting for transfers between devices, per_device(): lax.ppermute(got2, 'gy', [((i + k) % Y, i) for i in range(Y)])  1.39 us
  transfers between devices with their start and end apart: 2, of which 2 were waited for; matrix products, arithmetic and copies ran while one was open for 0% of the time, Pallas kernels for 2%

profile of v7, /device:TPU:0, one launch (start us, length us, event | category | flops | bytes accessed | tf_op | source)
XLA Modules:
  0.0 42.8 jit_solution(3037508954668731972)
XLA Ops:
  0.6 1.6 %shard_map.77 = (f32[32,1,128]{2,1,0:T(1,128)}, f32[112,128]{1,0:T(8,128)S(1)}, s32[24,128]{1,0:T(8,128)S(1)}) custom-call(f32[3,1,1,1,1536]{4,3,2,1,0:T(1,128)} %refs_0_.1, f32[3,1,1,1,1536]{4,3,2,1,0:T(1,128)} %refs_1_.1, f32[1,1,1,1536]{3,2,1,0:T(1,128)} %refs_2_.1, s32[1,1,1,1024]{3,2,1,0:T(1,128)} %refs_3_.1, s32[1,1,1,1024]{3,2,1,0:T(1,128)} %refs_4_.1, ...), custom_call_target="tpu_custom_call" | custom-call | tf_op jit(solution)/shard_map/pallas_call | solution.py:784
  2.2 7.3 %all-to-all-start = ((f32[32,1,128]{2,1,0:T(1,128)}), f32[32,1,128]{2,1,0:T(1,128)S(1)}, u32[]{:S(2)}, u32[]{:S(2)}) async-start(f32[32,1,128]{2,1,0:T(1,128)} %get-tuple-element.22), calls=%async_computation | async-start | bytes 32768 | tf_op jit(solution)/shard_map/all_to_all | solution.py:753
  9.6 0.9 %shard_map.78 = (s32[96,128]{1,0:T(8,128)S(1)}, f32[8,128]{1,0:T(8,128)S(1)}, f32[56,128]{1,0:T(8,128)S(1)}, f32[56,128]{1,0:T(8,128)S(1)}) custom-call(f32[112,128]{1,0:T(8,128)S(1)} %get-tuple-element.16.refs_0_, s32[24,128]{1,0:T(8,128)S(1)} %get-tuple-element.17.refs_1_), custom_call_target="tpu_custom_call" | custom-call | tf_op jit(solution)/shard_map/pallas_call | solution.py:784
  10.5 6.2 %all-to-all-done.refs_4_ = f32[32,1,128]{2,1,0:T(1,128)S(1)} async-done(((f32[32,1,128]{2,1,0:T(1,128)}), f32[32,1,128]{2,1,0:T(1,128)S(1)}, u32[]{:S(2)}, u32[]{:S(2)}) %all-to-all-start) | async-done | bytes 16416 | tf_op jit(solution)/shard_map/all_to_all | solution.py:753
  16.7 0.9 %shard_map.79 = (f32[136,128]{1,0:T(8,128)S(1)}, f32[32,10,1,128]{3,2,1,0:T(1,128)S(1)}) custom-call(s32[96,128]{1,0:T(8,128)S(1)} %get-tuple-element.18.refs_0_.refs_1_.refs_2_, f32[8,128]{1,0:T(8,128)S(1)} %get-tuple-element.19.refs_1_, f32[56,128]{1,0:T(8,128)S(1)} %get-tuple-element.20.refs_2_, f32[56,128]{1,0:T(8,128)S(1)} %get-tuple-element.21.refs_3_, ...), custom_call_target="tpu_custom_call" | custom-call | tf_op jit(solution)/shard_map/pallas_call | solution.py:784
  17.7 10.6 %all_to_all.15 = f32[32,10,1,128]{3,2,1,0:T(1,128)S(1)} all-to-all(f32[32,10,1,128]{3,2,1,0:T(1,128)S(1)} %get-tuple-element.24), channel_id=1, replica_groups=mesh['gx'=4,'gy'=2,'gz'=4] {'gx','gy','gz'}, dimensions={0} | all-to-all | bytes 327680 | tf_op jit(solution)/shard_map/all_to_all | solution.py:753
  28.2 0.0 collective-permute-start
  28.2 1.4 %collective-permute-done = f32[32,10,1,128]{3,2,1,0:T(1,128)S(1)} collective-permute-done((f32[32,10,1,128]{3,2,1,0:T(1,128)S(1)}, f32[32,10,1,128]{3,2,1,0:T(1,128)S(1)}, u32[]{:S(2)}, u32[]{:S(2)}) %collective-permute-start) | collective-permute-done | bytes 163872 | tf_op jit(solution)/shard_map/ppermute | solution.py:809
  29.6 1.6 %shard_map.80 = (f32[32,8,128]{2,1,0:T(8,128)S(1)}, f32[16,128]{1,0:T(8,128)S(1)}, f32[3,3,8,512]{3,2,1,0:T(8,128)S(1)}, f32[3,25,8,128]{3,2,1,0:T(8,128)S(1)}, f32[24,128]{1,0:T(8,128)S(1)}) custom-call(f32[136,128]{1,0:T(8,128)S(1)} %get-tuple-element.23.refs_0_.refs_1_, s32[96,128]{1,0:T(8,128)S(1)} %get-tuple-element.18.refs_0_.refs_1_.refs_2_, ...), custom_call_target="tpu_custom_call" | custom-call | tf_op jit(solution)/shard_map/pallas_call | solution.py:784
  31.2 10.1 %all_to_all.16 = f32[32,8,128]{2,1,0:T(8,128)S(1)} all-to-all(f32[32,8,128]{2,1,0:T(8,128)S(1)} %get-tuple-element.25), channel_id=1, replica_groups=mesh['gx'=4,'gy'=2,'gz'=4] {'gx','gy','gz'}, dimensions={0} | all-to-all | bytes 262144 | tf_op jit(solution)/shard_map/all_to_all | solution.py:753
  41.3 1.5 %shard_map.81 = (f32[3,1,1,1,1536]{4,3,2,1,0:T(1,128)}, f32[1,1,1,1024]{3,2,1,0:T(1,128)}) custom-call(f32[112,128]{1,0:T(8,128)S(1)} %get-tuple-element.16.refs_0_, f32[136,128]{1,0:T(8,128)S(1)} %get-tuple-element.23.refs_0_.refs_1_, s32[96,128]{1,0:T(8,128)S(1)} %get-tuple-element.18.refs_0_.refs_1_.refs_2_, f32[256,128]{1,0:T(8,128)S(1)} %bitcast.8, ...), custom_call_target="tpu_custom_call" | custom-call | tf_op jit(solution)/shard_map/pallas_call | solution.py:784
Async XLA Ops:
  2.2 14.5 %all-to-all-start = ((f32[32,1,128]{2,1,0:T(1,128)}), f32[32,1,128]{2,1,0:T(1,128)S(1)}, u32[]{:S(2)}, u32[]{:S(2)}) async-start(f32[32,1,128]{2,1,0:T(1,128)} %get-tuple-element.22), calls=%async_computation | async-start | bytes 32768 | tf_op jit(solution)/shard_map/all_to_all | solution.py:753
  28.2 1.4 %collective-permute-start = (f32[32,10,1,128]{3,2,1,0:T(1,128)S(1)}, f32[32,10,1,128]{3,2,1,0:T(1,128)S(1)}, u32[]{:S(2)}, u32[]{:S(2)}) collective-permute-start(f32[32,10,1,128]{3,2,1,0:T(1,128)S(1)} %all_to_all.15), channel_id=1, source_target_pairs={{4,0},{0,4},{5,1},{1,5},{6,2},{2,6},{7,3},{3,7},{12,8},{8,12},{13,... | collective-permute-start | bytes 491528 | tf_op jit(solution)/shard_map/ppermute | solution.py:809

commit v8 on v7

--- a/solution.py
+++ b/solution.py
@@ -91,7 +91,7 @@
 
 
 def send_kernel(size, old_hbm, move_hbm, mass_hbm, head_hbm, tail_hbm, send_hbm, out_ref, table, cons,
-                old_ref, move_ref, mass_ref, head_ref, tail_ref, send_ref, sems):
+                old_ref, move_ref, mass_ref, head_ref, tail_ref, send_ref, sems, out_vmem, out_sem):
     atom_rows = size["atom_rows"]
     send = size["send"]
     pad_rows = size["atom_pad"]
@@ -100,7 +100,7 @@
          (tail_hbm, tail_ref)])]
     for copy in copies:
         copy.start()
-    for copy in copies:
+    for copy in copies[:4]:
         copy.wait()
     table[...] = jnp.zeros(table.shape, F32)
     for r in range(atom_rows):
@@ -111,11 +111,8 @@
             table[a:a + 1, :] = old
             table[b:b + 1, :] = old + move_ref[d, 0, 0, 0, span].reshape(1, LANES)
     load_flat(mass_ref, (0, 0, 0), table, 6 * pad_rows, atom_rows)
-    load_flat(head_ref, (0, 0, 0), cons, 0, 8)
-    load_flat(tail_ref, (0, 0, 0), cons, 8, 8)
     lane = iota((pad_rows, LANES), 1)
     send_row = size["load_send"](send_ref)
-    cons[16:24, :] = jnp.broadcast_to(send_row, (8, LANES))
     index = jnp.broadcast_to(send_row, (pad_rows, LANES))
     low = index & 127
     hit = (index >> 7) == iota((pad_rows, LANES), 0)
@@ -125,7 +122,15 @@
         row = jnp.sum(got, axis=0, keepdims=True)
         message = jnp.where(lane[0:1] // send == q, row, message)
     for d in range(out_ref.shape[0]):
-        out_ref[d, :, :] = message
+        out_vmem[d, :, :] = message
+    leaving = pltpu.make_async_copy(out_vmem, out_ref, out_sem)
+    leaving.start()
+    for copy in copies[4:]:
+        copy.wait()
+    load_flat(head_ref, (0, 0, 0), cons, 0, 8)
+    load_flat(tail_ref, (0, 0, 0), cons, 8, 8)
+    cons[16:24, :] = jnp.broadcast_to(send_row, (8, LANES))
+    leaving.wait()
 
 
 def chain_sum(value, prev, extra):
@@ -777,14 +782,17 @@
                     map_row=NQ + (NQ + 1) // 2, load_send=load_send, start_lane=27 * send - 3 * LANES,
                     atom_parts=[min(8, atom_rows), max(atom_rows - 8, 0)])
 
-        def call(kernel, outs, scratch, *args, space=pltpu.VMEM):
+        def call(kernel, outs, scratch, *args, space=pltpu.VMEM, first_out=pltpu.VMEM):
+            first = jax.tree.leaves(outs)[0]
+
             def wrapped(*refs):
                 kernel(size, *refs)
 
             return pl.pallas_call(
                 wrapped, out_shape=outs, scratch_shapes=scratch,
                 in_specs=[pl.BlockSpec(memory_space=space)] * len(args),
-                out_specs=jax.tree.map(lambda _: pl.BlockSpec(memory_space=pltpu.VMEM), outs),
+                out_specs=jax.tree.map(
+                    lambda o: pl.BlockSpec(memory_space=first_out if o is first else pltpu.VMEM), outs),
                 compiler_params=pltpu.CompilerParams(vmem_limit_bytes=32 * 1024 * 1024),
             )(*[pltpu.with_memory_space_constraint(a, space) for a in args] if space == pltpu.HBM else args)
 
@@ -793,8 +801,9 @@
             send_kernel, (S((devices, 1, LANES), F32), S((7 * 16, LANES), F32), S((24, LANES), I32)),
             [pltpu.VMEM(old_pos.shape, F32), pltpu.VMEM(old_pos.shape, F32), pltpu.VMEM(inv_mass.shape, F32),
              pltpu.VMEM(bond_head.shape, I32), pltpu.VMEM(bond_tail.shape, I32), pltpu.VMEM(send_list.shape, I32),
-             pltpu.SemaphoreType.DMA((6,))],
-            old_pos, displacement, inv_mass, bond_head, bond_tail, send_list, space=pltpu.HBM)
+             pltpu.SemaphoreType.DMA((6,)), pltpu.VMEM((devices, 1, LANES), F32), pltpu.SemaphoreType.DMA],
+            old_pos, displacement, inv_mass, bond_head, bond_tail, send_list, space=pltpu.HBM,
+            first_out=pltpu.HBM)
         got1 = share(one)
         state_i, number, head_at, tail_at = call(
             map_kernel,

time: 43.1 us -> 43 us (level)
  no operation moved by 1% of the time
where the time goes in v8:
time: 43 us; the launch traced here: 42.8 us
  blocking collectives  20.7 us (48%)
  waiting for transfers between devices  7.58 us (18%)
  starting transfers between devices  7.33 us (17%)
  Pallas kernels  6.57 us (15%)
  between operations  0.67 us (2%)
    all_to_all x2, blocking collectives, share(): lax.all_to_all(message, AXES, split_axis=0, concat_axis=0, tiled=True)  20.7 us
    all_to_all x1, starting transfers between devices, share(): lax.all_to_all(message, AXES, split_axis=0, concat_axis=0, tiled=True)  7.33 us
    pallas_call x5, Pallas kernels, call(): pl.pallas_call(wrapped, out_shape=outs, scratch_shapes=scratch, in_specs=...  6.57 us
    all_to_all x1, waiting for transfers between devices, share(): lax.all_to_all(message, AXES, split_axis=0, concat_axis=0, tiled=True)  6.18 us
    ppermute x1, waiting for transfers between devices, per_device(): lax.ppermute(got2, 'gy', [((i + k) % Y, i) for i in range(Y)])  1.39 us
  transfers between devices with their start and end apart: 2, of which 2 were waited for; matrix products, arithmetic and copies ran while one was open for 0% of the time, Pallas kernels for 2%

profile of v8, /device:TPU:0, one launch (start us, length us, event | category | flops | bytes accessed | tf_op | source)
XLA Modules:
  0.0 42.8 jit_solution(17495648398498277883)
XLA Ops:
  0.6 1.6 %shard_map.77 = (f32[32,1,128]{2,1,0:T(1,128)}, f32[112,128]{1,0:T(8,128)S(1)}, s32[24,128]{1,0:T(8,128)S(1)}) custom-call(f32[3,1,1,1,1536]{4,3,2,1,0:T(1,128)} %refs_0_.1, f32[3,1,1,1,1536]{4,3,2,1,0:T(1,128)} %refs_1_.1, f32[1,1,1,1536]{3,2,1,0:T(1,128)} %refs_2_.1, s32[1,1,1,1024]{3,2,1,0:T(1,128)} %refs_3_.1, s32[1,1,1,1024]{3,2,1,0:T(1,128)} %refs_4_.1, ...), custom_call_target="tpu_custom_call" | custom-call | tf_op jit(solution)/shard_map/pallas_call | solution.py:791
  2.2 7.3 %all-to-all-start = ((f32[32,1,128]{2,1,0:T(1,128)}), f32[32,1,128]{2,1,0:T(1,128)S(1)}, u32[]{:S(2)}, u32[]{:S(2)}) async-start(f32[32,1,128]{2,1,0:T(1,128)} %get-tuple-element.22), calls=%async_computation | async-start | bytes 32768 | tf_op jit(solution)/shard_map/all_to_all | solution.py:758
  9.6 0.9 %shard_map.78 = (s32[96,128]{1,0:T(8,128)S(1)}, f32[8,128]{1,0:T(8,128)S(1)}, f32[56,128]{1,0:T(8,128)S(1)}, f32[56,128]{1,0:T(8,128)S(1)}) custom-call(f32[112,128]{1,0:T(8,128)S(1)} %get-tuple-element.16.refs_0_, s32[24,128]{1,0:T(8,128)S(1)} %get-tuple-element.17.refs_1_), custom_call_target="tpu_custom_call" | custom-call | tf_op jit(solution)/shard_map/pallas_call | solution.py:791
  10.5 6.2 %all-to-all-done.refs_4_ = f32[32,1,128]{2,1,0:T(1,128)S(1)} async-done(((f32[32,1,128]{2,1,0:T(1,128)}), f32[32,1,128]{2,1,0:T(1,128)S(1)}, u32[]{:S(2)}, u32[]{:S(2)}) %all-to-all-start) | async-done | bytes 16416 | tf_op jit(solution)/shard_map/all_to_all | solution.py:758
  16.7 0.9 %shard_map.79 = (f32[136,128]{1,0:T(8,128)S(1)}, f32[32,10,1,128]{3,2,1,0:T(1,128)S(1)}) custom-call(s32[96,128]{1,0:T(8,128)S(1)} %get-tuple-element.18.refs_0_.refs_1_.refs_2_, f32[8,128]{1,0:T(8,128)S(1)} %get-tuple-element.19.refs_1_, f32[56,128]{1,0:T(8,128)S(1)} %get-tuple-element.20.refs_2_, f32[56,128]{1,0:T(8,128)S(1)} %get-tuple-element.21.refs_3_, ...), custom_call_target="tpu_custom_call" | custom-call | tf_op jit(solution)/shard_map/pallas_call | solution.py:791
  17.6 10.6 %all_to_all.15 = f32[32,10,1,128]{3,2,1,0:T(1,128)S(1)} all-to-all(f32[32,10,1,128]{3,2,1,0:T(1,128)S(1)} %get-tuple-element.24), channel_id=1, replica_groups=mesh['gx'=4,'gy'=2,'gz'=4] {'gx','gy','gz'}, dimensions={0} | all-to-all | bytes 327680 | tf_op jit(solution)/shard_map/all_to_all | solution.py:758
  28.2 0.0 collective-permute-start
  28.2 1.4 %collective-permute-done = f32[32,10,1,128]{3,2,1,0:T(1,128)S(1)} collective-permute-done((f32[32,10,1,128]{3,2,1,0:T(1,128)S(1)}, f32[32,10,1,128]{3,2,1,0:T(1,128)S(1)}, u32[]{:S(2)}, u32[]{:S(2)}) %collective-permute-start) | collective-permute-done | bytes 163872 | tf_op jit(solution)/shard_map/ppermute | solution.py:818
  29.6 1.6 %shard_map.80 = (f32[32,8,128]{2,1,0:T(8,128)S(1)}, f32[16,128]{1,0:T(8,128)S(1)}, f32[3,3,8,512]{3,2,1,0:T(8,128)S(1)}, f32[3,25,8,128]{3,2,1,0:T(8,128)S(1)}, f32[24,128]{1,0:T(8,128)S(1)}) custom-call(f32[136,128]{1,0:T(8,128)S(1)} %get-tuple-element.23.refs_0_.refs_1_, s32[96,128]{1,0:T(8,128)S(1)} %get-tuple-element.18.refs_0_.refs_1_.refs_2_, ...), custom_call_target="tpu_custom_call" | custom-call | tf_op jit(solution)/shard_map/pallas_call | solution.py:791
  31.2 10.1 %all_to_all.16 = f32[32,8,128]{2,1,0:T(8,128)S(1)} all-to-all(f32[32,8,128]{2,1,0:T(8,128)S(1)} %get-tuple-element.25), channel_id=1, replica_groups=mesh['gx'=4,'gy'=2,'gz'=4] {'gx','gy','gz'}, dimensions={0} | all-to-all | bytes 262144 | tf_op jit(solution)/shard_map/all_to_all | solution.py:758
  41.3 1.5 %shard_map.81 = (f32[3,1,1,1,1536]{4,3,2,1,0:T(1,128)}, f32[1,1,1,1024]{3,2,1,0:T(1,128)}) custom-call(f32[112,128]{1,0:T(8,128)S(1)} %get-tuple-element.16.refs_0_, f32[136,128]{1,0:T(8,128)S(1)} %get-tuple-element.23.refs_0_.refs_1_, s32[96,128]{1,0:T(8,128)S(1)} %get-tuple-element.18.refs_0_.refs_1_.refs_2_, f32[256,128]{1,0:T(8,128)S(1)} %bitcast.8, ...), custom_call_target="tpu_custom_call" | custom-call | tf_op jit(solution)/shard_map/pallas_call | solution.py:791
Async XLA Ops:
  2.2 14.5 %all-to-all-start = ((f32[32,1,128]{2,1,0:T(1,128)}), f32[32,1,128]{2,1,0:T(1,128)S(1)}, u32[]{:S(2)}, u32[]{:S(2)}) async-start(f32[32,1,128]{2,1,0:T(1,128)} %get-tuple-element.22), calls=%async_computation | async-start | bytes 32768 | tf_op jit(solution)/shard_map/all_to_all | solution.py:758
  28.2 1.4 %collective-permute-start = (f32[32,10,1,128]{3,2,1,0:T(1,128)S(1)}, f32[32,10,1,128]{3,2,1,0:T(1,128)S(1)}, u32[]{:S(2)}, u32[]{:S(2)}) collective-permute-start(f32[32,10,1,128]{3,2,1,0:T(1,128)S(1)} %all_to_all.15), channel_id=1, source_target_pairs={{4,0},{0,4},{5,1},{1,5},{6,2},{2,6},{7,3},{3,7},{12,8},{8,12},{13,... | collective-permute-start | bytes 491528 | tf_op jit(solution)/shard_map/ppermute | solution.py:818
